TPU v7x, 256 devices: a whole 4x4x8 slice. The times are simulated.
256 devices in a mesh: lat: 8 (over x, z_hi), lon: 32 (over y, z_lo, core).
Axes of the slice: x: 4, y: 4, z: 8 (z_hi: 2, z_lo: 4; z = z_hi * 4 + z_lo), core: 2. Of those that a mesh axis runs over, the one named last changes fastest.
Arguments:
- tracers: float32 [100, 2, 128, 4096], P(None, None, 'lat', 'lon'), may hold values from 0.1 to 30, as said below
- offsets: int32 [2, 2, 128, 4096], P(None, None, 'lat', 'lon'), may hold values from -3 to 2
- target: float32 [100, 2, 128], P(None, None, 'lat'), may hold values from 0.3 to 4
- band_mask: int32 [128], P('lat'), may hold values 0 or 1
Outputs:
- nudged: float32 [100, 2, 128, 4096], P(None, None, 'lat', 'lon')
Inputs may be any that keep to these rules, and one draw needn't show every extreme that they name: Each cell's offsets are drawn independently of its neighbours', in both directions. `tracers`: positive mixing ratios.
All inputs are finite; a program needn't handle non-finite values. No bound on the sum of `band_mask` on one device may be relied on, other than what follows from the above.
Results may differ from a plain program's by a relative error of at most 0.00002.
Values sent between devices are 32-bit elements; how exact they have to be, the bound alone decides.
A program may use at most 64 MiB of HBM per device.

v0:
```python
import jax
import jax.numpy as jnp
from jax import lax
from jax.sharding import PartitionSpec as P

LON_TAPS = (-0.0546875, 0.8203125, 0.2734375, -0.0390625)
LAT_TAPS = (-0.0625, 0.5625, 0.5625, -0.0625)


def extended(value, sides, width, wrap):
    for axis, dim in sides:
        size, length = (lax.axis_size(axis), value.shape[dim])
        up = [(i, (i + 1) % size) for i in range(size if wrap else size - 1)]
        down = [(j, i) for i, j in up]
        last = lax.slice_in_dim(value, length - width, length, axis=dim)
        leading = lax.slice_in_dim(value, 0, width, axis=dim)
        before = lax.ppermute(last, axis, up)
        after = lax.ppermute(leading, axis, down)
        value = jnp.concatenate([before, value, after], axis=dim)
    return value


def from_everyone(value, axis):
    length = lax.axis_size(axis)
    return lax.all_to_all(
        jnp.broadcast_to(value[None], (length, *value.shape)), axis, 0, 0, tiled=True
    )


def over_copies(value, axis):
    return from_everyone(value, axis).sum(axis=0)


def reach_weights(offset, taps):
    weights = [jnp.zeros(offset.shape, jnp.float32) for index in range(9)]
    for shift in range(-3, 3):
        matches = (offset == shift).astype(jnp.float32)
        for tap in range(4):
            where_to = shift + tap - 1 + 4
            weights[where_to] = weights[where_to] + taps[tap] * matches
    return weights


def stencil(padded, lon_weights, lat_weights, rows, cols):
    total_sum = jnp.zeros(padded.shape[:-2] + (rows, cols), jnp.float32)
    for row_shift in range(9):
        row_part = padded[..., row_shift : row_shift + rows, :]
        inner = jnp.zeros_like(total_sum)
        for col_shift in range(9):
            inner = inner + lon_weights[col_shift] * row_part[..., col_shift : col_shift + cols]
        total_sum = total_sum + lat_weights[row_shift] * inner
    return total_sum


def body(tracers, offsets, target, band_mask):
    rows = tracers.shape[2]
    cols = tracers.shape[3]
    widened = extended(tracers, (("lon", 3),), 4, True)
    padded = extended(widened, (("lat", 2),), 4, False)
    lon_weights = reach_weights(offsets[0], LON_TAPS)
    lat_weights = reach_weights(offsets[1], LAT_TAPS)
    advected = stencil(padded, lon_weights, lat_weights, rows, cols)
    squares = jnp.sum(advected * advected, axis=-1)
    columns_all = cols * lax.axis_size("lon")
    mask_rows = band_mask.astype(jnp.float32)
    totals = over_copies(squares, "lon")
    rms = jnp.sqrt(totals / columns_all + 1e-06)
    factor = 1.0 + 0.5 * mask_rows[None, None, :] * (target / rms - 1.0)
    return advected * factor[..., None]


def solution(mesh):
    placed = (
        P(None, None, "lat", "lon"),
        P(None, None, "lat", "lon"),
        P(None, None, "lat"),
        P("lat"),
    )
    return jax.shard_map(
        body, mesh=mesh, in_specs=placed, out_specs=P(None, None, "lat", "lon"), check_vma=False
    )
```

profile of v0, /device:TPU:1, one launch (start us, length us, event | category | flops | bytes accessed | tf_op | source)
XLA Modules:
  0.0 151.7 jit_solution(9687334393300068748)
XLA Ops:
  0.0 2.5 %fusion.111 = (f32[100,2,16,4]{3,2,1,0:T(8,128)S(1)}, f32[100,2,16,4]{3,2,1,0:T(8,128)S(1)}) fusion(f32[100,2,16,128]{3,2,1,0:T(8,128)} %param.4), kind=kLoop, calls=%fused_computation.239 | loop fusion | bytes 204800 | tf_op jit(solution)/shard_map/slice | solution.py:15
  2.5 0.0 copy-start.2
  2.5 1.1 copy.18
  3.6 3.2 %collective-permute-start.1 = (f32[100,2,16,4]{0,2,3,1:T(8,128)S(1)}, f32[100,2,16,4]{0,2,3,1:T(8,128)S(1)}, u32[]{:S(2)}, u32[]{:S(2)}) collective-permute-start(f32[100,2,16,4]{0,2,3,1:T(8,128)S(1)} %copy.18), channel_id=1, source_target_pairs={{1,0},{2,1},{3,2},{4,3},{5,4},{6,5},{7,6},{8,7},{9,8},{10,9},{11,1... | collective-permute-start | bytes 153608 | tf_op jit(solution)/shard_map/ppermute | solution.py:18
  6.9 1.1 copy.17
  7.9 0.0 collective-permute-start
  8.0 0.0 copy-done.2
  8.2 1.9 %copy.9 = f32[100,2,16,128]{0,3,2,1:T(8,128)S(1)} copy(f32[100,2,16,128]{3,2,1,0:T(8,128)} %param.4) | data formatting | bytes 3276800 | tf_op args[0]
  10.1 0.0 copy-start
  10.1 0.0 collective-permute-done.1
  10.2 3.3 %collective-permute-done = f32[100,2,16,4]{0,2,3,1:T(8,128)S(1)} collective-permute-done((f32[100,2,16,4]{0,2,3,1:T(8,128)S(1)}, f32[100,2,16,4]{0,2,3,1:T(8,128)S(1)}, u32[]{:S(2)}, u32[]{:S(2)}) %collective-permute-start) | collective-permute-done | bytes 51232 | tf_op jit(solution)/shard_map/ppermute | solution.py:17
  13.6 0.1 pad_maximum_fusion.5
  13.7 6.2 %collective-permute-start.2 = (f32[100,2,4,136]{0,3,2,1:T(8,128)S(1)}, f32[100,2,4,136]{0,3,2,1:T(8,128)S(1)}, u32[]{:S(2)}, u32[]{:S(2)}) collective-permute-start(f32[100,2,4,136]{0,3,2,1:T(8,128)S(1)} %get-tuple-element.33), channel_id=1, source_target_pairs={{0,32},{32,64},{64,96},{96,128},{128,160},{160,192},{192,224},{1,3... | collective-permute-start | bytes 1305608 | tf_op jit(solution)/shard_map/ppermute | solution.py:17
  19.9 1.3 collective-permute-start.3
  21.2 23.5 %collective-permute-done.2 = f32[100,2,4,136]{0,3,2,1:T(8,128)S(1)} collective-permute-done((f32[100,2,4,136]{0,3,2,1:T(8,128)S(1)}, f32[100,2,4,136]{0,3,2,1:T(8,128)S(1)}, u32[]{:S(2)}, u32[]{:S(2)}) %collective-permute-start.2) | collective-permute-done | bytes 435232 | tf_op jit(solution)/shard_map/ppermute | solution.py:17
  44.7 0.0 copy-done
  44.7 12.3 %collective-permute-done.3 = f32[100,2,4,136]{0,3,2,1:T(8,128)S(1)} collective-permute-done((f32[100,2,4,136]{0,3,2,1:T(8,128)S(1)}, f32[100,2,4,136]{0,3,2,1:T(8,128)S(1)}, u32[]{:S(2)}, u32[]{:S(2)}) %collective-permute-start.3) | collective-permute-done | bytes 435232 | tf_op jit(solution)/shard_map/ppermute | solution.py:18
  57.0 4.1 %maximum_maximum_fusion = (f32[100,2,20,136]{0,3,2,1:T(8,128)S(1)}, f32[100,2,20,136]{0,3,2,1:T(8,128)}) fusion(f32[100,2,16,4]{0,3,2,1:T(4,128)S(1)} %copy.10, f32[100,2,16,128]{0,3,2,1:T(8,128)} %copy-done, f32[100,2,16,4]{0,3,2,1:T(4,128)S(1)} %copy.8, f32[100,2,4,136]{0,3,2,1:T(8,128)S(1)} %collective-permute-done.2, ...), kind=kLoop, calls=%fused_computation.6 | loop fusion | flops 3264000 | bytes 6963200 | tf_op jit(solution)/shard_map/concatenate | solution.py:19
  61.1 0.0 copy-start.4
  61.1 50.2 %multiply_reduce_fusion = (f32[100,2,16]{0,2,1:T(8,128)S(1)}, f32[100,2,16,128]{0,3,2,1:T(8,128)}) fusion(f32[100,2,20,136]{0,3,2,1:T(8,128)} %get-tuple-element.32, f32[2,16,128]{2,1,0:T(8,128)S(1)} %get-tuple-element.46, f32[2,16,128]{2,1,0:T(8,128)S(1)} %get-tuple-element.44, f32[2,16,128]{2,1,0:T(8,128)S(1)} %get-tuple-element.43, ...), kind=kLoop, calls=%fused_computation.187 | loop fusion | flops 73724800 | bytes 121651712 | tf_op jit(solution)/shard_map/reduce_sum | solution.py:63
  111.3 0.0 copy-start.3
  111.3 0.0 copy-start.1
  111.3 0.9 broadcast_in_dim.2
  112.2 18.1 %all-to-all-start = ((f32[32,100,2,16]{1,3,2,0:T(8,128)}), f32[32,100,2,16]{1,3,2,0:T(8,128)S(1)}, u32[]{:S(2)}, u32[]{:S(2)}) async-start(f32[32,100,2,16]{1,3,2,0:T(8,128)} %broadcast_in_dim.2), calls=%async_computation | async-start | bytes 1048576 | tf_op jit(solution)/shard_map/all_to_all | solution.py:25
  130.3 0.0 copy-done.4
  130.3 16.8 %all-to-all-done = f32[32,100,2,16]{1,3,2,0:T(8,128)S(1)} async-done(((f32[32,100,2,16]{1,3,2,0:T(8,128)}), f32[32,100,2,16]{1,3,2,0:T(8,128)S(1)}, u32[]{:S(2)}, u32[]{:S(2)}) %all-to-all-start) | async-done | bytes 409632 | tf_op jit(solution)/shard_map/all_to_all | solution.py:25
  147.0 0.1 reduce_sum.19
  147.1 0.0 copy-done.3
  147.1 0.1 multiply_add_fusion
  147.2 0.0 copy-done.1
  147.2 1.5 %broadcast_multiply_fusion = f32[100,2,16,128]{0,3,2,1:T(8,128)} fusion(f32[100,2,16,128]{0,3,2,1:T(8,128)S(1)} %copy-done.1, f32[100,2,16]{0,2,1:T(8,128)S(1)} %multiply_add_fusion), kind=kLoop, calls=%fused_computation.188 | loop fusion | flops 409600 | bytes 3289600 | tf_op jit(solution)/shard_map/mul | solution.py:69
  148.7 3.0 %copy.16 = f32[100,2,16,128]{3,2,1,0:T(8,128)} copy(f32[100,2,16,128]{0,3,2,1:T(8,128)} %broadcast_multiply_fusion) | data formatting | bytes 3276800 | tf_op jit(solution)/shard_map/mul | solution.py:69
  (14 shorter events, 0.2 us)
Async XLA Ops:
  2.5 5.5 %copy-start.2 = (s32[2,2,16,128]{3,2,1,0:T(8,128)S(1)}, s32[2,2,16,128]{3,2,1,0:T(8,128)}, u32[]{:S(2)}) copy-start(s32[2,2,16,128]{3,2,1,0:T(8,128)} %param.5) | copy-start | bytes 98308
  3.6 6.5 %collective-permute-start.1 = (f32[100,2,16,4]{0,2,3,1:T(8,128)S(1)}, f32[100,2,16,4]{0,2,3,1:T(8,128)S(1)}, u32[]{:S(2)}, u32[]{:S(2)}) collective-permute-start(f32[100,2,16,4]{0,2,3,1:T(8,128)S(1)} %copy.18), channel_id=1, source_target_pairs={{1,0},{2,1},{3,2},{4,3},{5,4},{6,5},{7,6},{8,7},{9,8},{10,9},{11,1... | collective-permute-start | bytes 153608 | tf_op jit(solution)/shard_map/ppermute | solution.py:18
  7.9 5.6 %collective-permute-start = (f32[100,2,16,4]{0,2,3,1:T(8,128)S(1)}, f32[100,2,16,4]{0,2,3,1:T(8,128)S(1)}, u32[]{:S(2)}, u32[]{:S(2)}) collective-permute-start(f32[100,2,16,4]{0,2,3,1:T(8,128)S(1)} %copy.17), channel_id=1, source_target_pairs={{0,1},{1,2},{2,3},{3,4},{4,5},{5,6},{6,7},{7,8},{8,9},{9,10},{10,1... | collective-permute-start | bytes 153608 | tf_op jit(solution)/shard_map/ppermute | solution.py:17
  10.1 34.6 %copy-start = (f32[100,2,16,128]{0,3,2,1:T(8,128)}, f32[100,2,16,128]{0,3,2,1:T(8,128)S(1)}, u32[]{:S(2)}) copy-start(f32[100,2,16,128]{0,3,2,1:T(8,128)S(1)} %copy.9) | copy-start | bytes 4915204
  13.7 31.0 %collective-permute-start.2 = (f32[100,2,4,136]{0,3,2,1:T(8,128)S(1)}, f32[100,2,4,136]{0,3,2,1:T(8,128)S(1)}, u32[]{:S(2)}, u32[]{:S(2)}) collective-permute-start(f32[100,2,4,136]{0,3,2,1:T(8,128)S(1)} %get-tuple-element.33), channel_id=1, source_target_pairs={{0,32},{32,64},{64,96},{96,128},{128,160},{160,192},{192,224},{1,3... | collective-permute-start | bytes 1305608 | tf_op jit(solution)/shard_map/ppermute | solution.py:17
  19.9 37.1 %collective-permute-start.3 = (f32[100,2,4,136]{0,3,2,1:T(8,128)S(1)}, f32[100,2,4,136]{0,3,2,1:T(8,128)S(1)}, u32[]{:S(2)}, u32[]{:S(2)}) collective-permute-start(f32[100,2,4,136]{0,3,2,1:T(8,128)S(1)} %get-tuple-element.34), channel_id=1, source_target_pairs={{32,0},{64,32},{96,64},{128,96},{160,128},{192,160},{224,192},{33,... | collective-permute-start | bytes 1305608 | tf_op jit(solution)/shard_map/ppermute | solution.py:18
  61.1 69.2 %copy-start.4 = (s32[16]{0:T(128)S(1)}, s32[16]{0:T(128)}, u32[]{:S(2)}) copy-start(s32[16]{0:T(128)} %param.7) | copy-start | bytes 196
  111.3 35.8 %copy-start.3 = (f32[100,2,16]{0,2,1:T(8,128)S(1)}, f32[100,2,16]{0,2,1:T(8,128)}, u32[]{:S(2)}) copy-start(f32[100,2,16]{0,2,1:T(8,128)} %param.6) | copy-start | bytes 38404
  111.3 35.9 %copy-start.1 = (f32[100,2,16,128]{0,3,2,1:T(8,128)S(1)}, f32[100,2,16,128]{0,3,2,1:T(8,128)}, u32[]{:S(2)}) copy-start(f32[100,2,16,128]{0,3,2,1:T(8,128)} %get-tuple-element.6) | copy-start | bytes 4915204
  112.2 34.9 %all-to-all-start = ((f32[32,100,2,16]{1,3,2,0:T(8,128)}), f32[32,100,2,16]{1,3,2,0:T(8,128)S(1)}, u32[]{:S(2)}, u32[]{:S(2)}) async-start(f32[32,100,2,16]{1,3,2,0:T(8,128)} %broadcast_in_dim.2), calls=%async_computation | async-start | bytes 1048576 | tf_op jit(solution)/shard_map/all_to_all | solution.py:25
where the time goes:
time: 153 us; the launch traced here: 152 us
  other arithmetic  56.3 us (37%)
  waiting for transfers between devices  55.9 us (37%)
  starting transfers between devices  28.8 us (19%)
  local copies, waits for them, and re-layouts  10.5 us (7%)
    reduce_sum x1, other arithmetic, body(): squares = jnp.sum(advected * advected, axis=-1)  50.2 us
    ppermute x2, waiting for transfers between devices, extended(): before = lax.ppermute(last, axis, up)  26.9 us
    all_to_all x1, starting transfers between devices, from_everyone(): lax.all_to_all(jnp.broadcast_to(value[None], (length, *value.shape)), axi...  18.1 us
    all_to_all x1, waiting for transfers between devices, from_everyone(): lax.all_to_all(jnp.broadcast_to(value[None], (length, *value.shape)), axi...  16.8 us
    ppermute x2, waiting for transfers between devices, extended(): after = lax.ppermute(leading, axis, down)  12.3 us
    ppermute x2, starting transfers between devices, extended(): before = lax.ppermute(last, axis, up)  6.19 us
    ppermute x2, starting transfers between devices, extended(): after = lax.ppermute(leading, axis, down)  4.53 us
    unnamed x13, local copies, waits for them, and re-layouts  4.12 us
  transfers between devices with their start and end apart: 5, of which 4 were waited for; matrix products, arithmetic and copies ran while one was open for 2% of the time, Pallas kernels for 0%

commit v1 on v0

v1 whole, which is shorter than its diff:
```python
import functools

import jax
import jax.numpy as jnp
from jax import lax
from jax.experimental import pallas as pl
from jax.experimental.pallas import tpu as pltpu
from jax.sharding import PartitionSpec as P

LON_TAPS = (-0.0546875, 0.8203125, 0.2734375, -0.0390625)
LAT_TAPS = (-0.0625, 0.5625, 0.5625, -0.0625)
MESH = pl.DeviceIdType.MESH
F32 = jnp.float32
BF16 = jnp.bfloat16
TP = 112
KW = 384
BANDS = 24
ZGROUP = 4
CORES = 2


def tap_select(distance, taps):
    out = jnp.zeros(distance.shape, F32)
    for k in range(4):
        out = jnp.where(distance == k - 1, taps[k], out)
    return out


def lon_matrix(o0, lcat):
    rows = lax.broadcasted_iota(jnp.int32, (128, 128), 0)
    lanes = lax.broadcasted_iota(jnp.int32, (128, 128), 1)
    main = tap_select(rows - lanes - o0, LON_TAPS).astype(BF16)
    lcat[0:128, :] = main
    lcat[128:256, :] = main
    e = lax.broadcasted_iota(jnp.int32, (16, 128), 0) % 8
    lanes = lax.broadcasted_iota(jnp.int32, (16, 128), 1)
    edge = jnp.where(e < 4, e - 4, e + 124)
    lcat[256:272, :] = tap_select(edge - lanes - o0, LON_TAPS).astype(BF16)


def kernel(nt, nlat, nlon, x_hbm, off_hbm, target_ref, mask_ref, out_ref,
           xv, xb, offv, es, er, ob, zs, zr, acc, lcat, sums, sums_t, ra, rb,
           local_sem, e_send, e_recv, o_send, o_recv, z_send, z_recv, a_send, a_recv, b_send, b_recv):
    lat = lax.axis_index("lat")
    lon = lax.axis_index("lon")
    left = lax.rem(lon + nlon - 1, nlon)
    right = lax.rem(lon + 1, nlon)
    core = lax.rem(lon, CORES)
    zlo = lax.rem(lon // CORES, ZGROUP)
    ny = nlon // (ZGROUP * CORES)
    yy = lon // (ZGROUP * CORES)

    load_x = pltpu.make_async_copy(x_hbm, xv.at[pl.ds(0, nt * 32)], local_sem.at[0])
    load_x.start()
    load_off = pltpu.make_async_copy(off_hbm, offv, local_sem.at[1])
    load_off.start()

    def z_peer(k):
        return {"lon": (yy * ZGROUP + lax.rem(zlo + k, ZGROUP)) * CORES + core}

    def y_peer(k):
        me = yy * CORES + core
        other = lax.rem(me + k, ny * CORES)
        return {"lon": ((other // CORES) * ZGROUP + zlo) * CORES + lax.rem(other, CORES)}

    barrier = pltpu.get_barrier_semaphore()

    def greet(device):
        pl.semaphore_signal(barrier, inc=1, device_id=device, device_id_type=MESH)

    has_up = lat > 0
    has_down = lat < nlat - 1

    @pl.when(has_up)
    def _():
        greet({"lat": lat - 1})

    @pl.when(has_down)
    def _():
        greet({"lat": lat + 1})

    greet({"lon": left})
    greet({"lon": right})
    for k in range(1, ZGROUP):
        greet(z_peer(k))
    for k in range(1, ny * CORES):
        greet(y_peer(k))

    xv[pl.ds(nt * 32, (TP - nt) * 32), :] = jnp.zeros(((TP - nt) * 32, 128), F32)
    for l in range(2):
        for first in (0, 20):
            xb[pl.ds((l * BANDS + first) * TP, 4 * TP), :] = jnp.zeros((4 * TP, KW), BF16)
    lcat[272:384, :] = jnp.zeros((112, 128), BF16)
    lane = lax.broadcasted_iota(jnp.int32, (TP, 128), 1)

    load_off.wait()
    load_x.wait()

    def pack(lj, carry):
        to_left, to_right = carry
        v = xv[pl.ds(lj, TP, stride=32), :]
        rolled = pltpu.roll(v, 4 * lj, 1)
        group = lane // 4
        to_left = jnp.where(group == lj, rolled, to_left)
        to_right = jnp.where(group == lax.rem(lj + 31, 32), rolled, to_right)
        hi = v.astype(BF16)
        lo = (v - hi.astype(F32)).astype(BF16)
        row = pl.multiple_of(((lj // 16) * BANDS + 4 + lax.rem(lj, 16)) * TP, 16)
        xb[pl.ds(row, TP), 0:128] = hi
        xb[pl.ds(row, TP), 128:256] = lo
        return to_left, to_right

    zero = jnp.zeros((TP, 128), F32)
    to_left, to_right = lax.fori_loop(0, 32, pack, (zero, zero))
    es[0] = to_left
    es[1] = to_right

    pl.semaphore_wait(
        barrier, has_up.astype(jnp.int32) + has_down.astype(jnp.int32) + 2 + (ZGROUP - 1) + (ny * CORES - 1)
    )

    def o_copy(direction):
        return pltpu.make_async_remote_copy(
            src_ref=offv.reshape(2, 2, 16, 128).at[:, :, pl.ds(12 * direction, 4), :],
            dst_ref=ob.at[direction],
            send_sem=o_send.at[direction], recv_sem=o_recv.at[direction],
            device_id={"lat": lat - 1 + 2 * direction}, device_id_type=MESH)

    def e_copy(side):
        return pltpu.make_async_remote_copy(
            src_ref=es.at[side], dst_ref=er.at[1 - side],
            send_sem=e_send.at[side], recv_sem=e_recv.at[1 - side],
            device_id={"lon": left if side == 0 else right}, device_id_type=MESH)

    def z_copy(direction, s):
        return pltpu.make_async_remote_copy(
            src_ref=zs.at[direction, s, pl.ds(0, nt)], dst_ref=zr.at[direction, s, pl.ds(0, nt)],
            send_sem=z_send.at[direction, s], recv_sem=z_recv.at[direction, s],
            device_id={"lat": lat + 1 - 2 * direction}, device_id_type=MESH)

    @pl.when(has_up)
    def _():
        o_copy(0).start()

    @pl.when(has_down)
    def _():
        o_copy(1).start()

    e_copy(0).start()
    e_copy(1).start()
    for side in range(2):
        pltpu.make_async_remote_copy(
            src_ref=es.at[side], dst_ref=er.at[side], send_sem=e_send.at[side], recv_sem=e_recv.at[side],
            device_id={"lon": left}, device_id_type=MESH).wait_recv()

    def edges(lj, _):
        shift = lax.rem(132 - 4 * lj, 128)
        a = pltpu.roll(er[0], shift, 1)
        b = pltpu.roll(er[1], shift, 1)
        e = jnp.where(lane < 4, a, b)
        hi = e.astype(BF16).astype(F32)
        both = jnp.where(lane < 8, hi, pltpu.roll(e - hi, 8, 1))
        row = pl.multiple_of(((lj // 16) * BANDS + 4 + lax.rem(lj, 16)) * TP, 16)
        xb[pl.ds(row, TP), 256:384] = both.astype(BF16)
        return 0

    lax.fori_loop(0, 32, edges, 0)

    for direction in range(2):
        exists = has_down if direction == 0 else has_up

        @pl.when(exists)
        def _():
            pltpu.make_async_remote_copy(
                src_ref=ob.at[direction], dst_ref=ob.at[direction],
                send_sem=o_send.at[direction], recv_sem=o_recv.at[direction],
                device_id={"lat": lat + 1 - 2 * direction}, device_id_type=MESH).wait_recv()

            def part(s, _):
                l, jj = s // 4, lax.rem(s, 4)
                o0 = ob[direction, 0, l, pl.ds(jj, 1), :]
                o1 = ob[direction, 1, l, pl.ds(jj, 1), :]
                lon_matrix(o0, lcat)
                start = pl.multiple_of((l * BANDS + 4 + 12 * (1 - direction)) * TP, 16)
                y = jnp.dot(xb[pl.ds(start, 4 * TP), :], lcat[...], preferred_element_type=F32)
                total = jnp.zeros((TP, 128), F32)
                for hh in range(4):
                    w = tap_select(hh + (4 if direction else -4) - jj - o1, LAT_TAPS)
                    total = total + w * y[hh * TP:(hh + 1) * TP]
                zs[direction, s] = total
                z_copy(direction, s).start()
                return 0

            lax.fori_loop(0, 8, part, 0)

    def own(lj, _):
        l, j = lj // 16, lax.rem(lj, 16)
        o0 = offv[pl.ds(lj, 1), :]
        o1 = offv[pl.ds(32 + lj, 1), :]
        lon_matrix(o0, lcat)
        start = pl.multiple_of((l * BANDS + j) * TP, 16)
        y = jnp.dot(xb[pl.ds(start, 9 * TP), :], lcat[...], preferred_element_type=F32)
        total = jnp.zeros((TP, 128), F32)
        for rr in range(9):
            w = tap_select(rr - 4 - o1, LAT_TAPS)
            total = total + w * y[rr * TP:(rr + 1) * TP]
        acc[lj] = total
        return 0

    lax.fori_loop(0, 32, own, 0)

    for direction in range(2):
        exists = has_up if direction == 0 else has_down

        @pl.when(exists)
        def _():
            def add(s, _):
                z_copy(direction, s).wait_recv()
                lj = (s // 4) * 16 + 12 * direction + lax.rem(s, 4)
                acc[lj] = acc[lj] + zr[direction, s]
                return 0

            lax.fori_loop(0, 8, add, 0)

    def square(lj, total):
        a = acc[lj]
        return jnp.where(lane == lj, jnp.sum(a * a, axis=1, keepdims=True), total)

    sums[0:TP, :] = lax.fori_loop(0, 32, square, zero)
    sums[TP:128, :] = jnp.zeros((128 - TP, 128), F32)
    sums_t[...] = jnp.transpose(sums[...])[0:32]

    def exchange(peer, group, me, slots, send, recv, src):
        copies = []
        for k in range(1, group):
            copies.append(pltpu.make_async_remote_copy(
                src_ref=src, dst_ref=slots.at[k], send_sem=send.at[k], recv_sem=recv.at[k],
                device_id=peer(k), device_id_type=MESH))
        for c in copies:
            c.start()
        total = src[...]
        for k, c in enumerate(copies):
            c.wait_recv()
            total = total + slots[k + 1]
        return total, copies

    total, a_copies = exchange(z_peer, ZGROUP, zlo, ra, a_send, a_recv, sums_t)
    ra[0] = total
    total, b_copies = exchange(y_peer, ny * CORES, 0, rb, b_send, b_recv, ra.at[0])

    rms = jnp.sqrt(total * (1.0 / (128 * nlon)) + 1e-06)
    row = lax.rem(lax.broadcasted_iota(jnp.int32, (32, 128), 0), 16)
    mask = jnp.zeros((32, 128), F32)
    for j in range(16):
        mask = jnp.where(row == j, mask_ref[j].astype(F32), mask)
    factor = 1.0 + 0.5 * mask * (target_ref[...] / rms - 1.0)
    sums[0:32, :] = factor
    factor_t = jnp.transpose(sums[...])[0:TP]

    def scale(lj, _):
        column = jnp.sum(jnp.where(lane == lj, factor_t, 0.0), axis=1, keepdims=True)
        out_ref[pl.ds(lj, nt, stride=32), :] = (acc[lj] * column)[0:nt]
        return 0

    lax.fori_loop(0, 32, scale, 0)

    e_copy(0).wait_send()
    e_copy(1).wait_send()
    for c in a_copies + b_copies:
        c.wait_send()
    for direction in range(2):
        exists = has_down if direction == 0 else has_up

        @pl.when(exists)
        def _():
            o_copy(1 - direction).wait_send()
            lax.fori_loop(0, 8, lambda s, _: (z_copy(direction, s).wait_send(), 0)[1], 0)


def solution(mesh):
    nlat, nlon = mesh.shape["lat"], mesh.shape["lon"]

    def body(tracers, offsets, target, band_mask):
        nt = tracers.shape[0]
        nb = nlon // ZGROUP
        target_t = jnp.pad(jnp.transpose(target, (1, 2, 0)).reshape(32, nt), ((0, 0), (0, 128 - nt)), constant_values=1.0)
        vmem = pltpu.VMEM
        out = pl.pallas_call(
            functools.partial(kernel, nt, nlat, nlon),
            out_shape=jax.ShapeDtypeStruct((nt * 32, 128), F32),
            in_specs=[
                pl.BlockSpec(memory_space=pl.ANY),
                pl.BlockSpec(memory_space=pl.ANY),
                pl.BlockSpec(memory_space=pltpu.VMEM),
                pl.BlockSpec(memory_space=pltpu.SMEM),
            ],
            out_specs=pl.BlockSpec(memory_space=pltpu.VMEM),
            scratch_shapes=[
                vmem((TP * 32, 128), F32),
                vmem((2 * BANDS * TP, KW), BF16),
                vmem((64, 128), jnp.int32),
                vmem((2, TP, 128), F32),
                vmem((2, TP, 128), F32),
                vmem((2, 2, 2, 4, 128), jnp.int32),
                vmem((2, 8, TP, 128), F32),
                vmem((2, 8, TP, 128), F32),
                vmem((32, TP, 128), F32),
                vmem((KW, 128), BF16),
                vmem((128, 128), F32),
                vmem((32, 128), F32),
                vmem((ZGROUP, 32, 128), F32),
                vmem((nb, 32, 128), F32),
                pltpu.SemaphoreType.DMA((2,)),
                pltpu.SemaphoreType.DMA((2,)),
                pltpu.SemaphoreType.DMA((2,)),
                pltpu.SemaphoreType.DMA((2,)),
                pltpu.SemaphoreType.DMA((2,)),
                pltpu.SemaphoreType.DMA((2, 8)),
                pltpu.SemaphoreType.DMA((2, 8)),
                pltpu.SemaphoreType.DMA((ZGROUP,)),
                pltpu.SemaphoreType.DMA((ZGROUP,)),
                pltpu.SemaphoreType.DMA((nb,)),
                pltpu.SemaphoreType.DMA((nb,)),
            ],
            compiler_params=pltpu.CompilerParams(
                collective_id=0, has_side_effects=True, vmem_limit_bytes=48 * 1024 * 1024
            ),
        )(tracers.reshape(nt * 32, 128), offsets.reshape(64, 128), target_t, band_mask)
        return out.reshape(tracers.shape)

    placed = (
        P(None, None, "lat", "lon"),
        P(None, None, "lat", "lon"),
        P(None, None, "lat"),
        P("lat"),
    )
    return jax.shard_map(
        body, mesh=mesh, in_specs=placed, out_specs=P(None, None, "lat", "lon"), check_vma=False
    )
```

time: 153 us -> 79.9 us (0.52)
  Pallas kernels: 0 us -> 74.9 us
  other arithmetic: 56.3 us -> 0 us
  waiting for transfers between devices: 55.9 us -> 0 us
  starting transfers between devices: 28.8 us -> 0 us
  local copies, waits for them, and re-layouts: 10.5 us -> 4.73 us
    pallas_call x0 -> x1, Pallas kernels: none -> 74.9 us  [body(): pl.pallas_call(functools.partial(kernel, nt, nlat, nlon), out_shape=jax.S...]
    reduce_sum x2 -> x0, other arithmetic: 50.3 us -> none  [the longest x1 50.2 us: body(): squares = jnp.sum(advected * advected, axis=-1)]
    ppermute x4 -> x0, waiting for transfers between devices: 39.1 us -> none  [the longest x2 26.9 us: extended(): before = lax.ppermute(last, axis, up)]
    all_to_all x1 -> x0, starting transfers between devices: 18.1 us -> none  [from_everyone(): lax.all_to_all(jnp.broadcast_to(value[None], (length, *value.shape)), axi...]
    all_to_all x1 -> x0, waiting for transfers between devices: 16.8 us -> none  [from_everyone(): lax.all_to_all(jnp.broadcast_to(value[None], (length, *value.shape)), axi...]
    ppermute x4 -> x0, starting transfers between devices: 10.7 us -> none  [the longest x2 6.19 us: extended(): before = lax.ppermute(last, axis, up)]
    concatenate x1 -> x0, other arithmetic: 4.09 us -> none  [extended(): value = jnp.concatenate([before, value, after], axis=dim)]
    mul x1 -> x0, local copies, waits for them, and re-layouts: 2.96 us -> none  [body(): return advected * factor[..., None]]
  transfers between devices with their start and end apart: 5 -> 0, of which waited for: 4 -> 0; matrix products, arithmetic and copies ran while one was open for 2% -> 0% of each run, Pallas kernels for 0% -> 0%
where the time goes in v1:
time: 79.9 us; the launch traced here: 79.7 us
  Pallas kernels  74.9 us (94%)
  local copies, waits for them, and re-layouts  4.73 us (6%)
    pallas_call x1, Pallas kernels, body(): pl.pallas_call(functools.partial(kernel, nt, nlat, nlon), out_shape=jax.S...  74.9 us
    unnamed x7, local copies, waits for them, and re-layouts  4.01 us

profile of v1, /device:TPU:1, one launch (start us, length us, event | category | flops | bytes accessed | tf_op | source)
XLA Modules:
  0.0 79.7 jit_solution(13139858599353750629)
XLA Ops:
  0.0 0.7 pad.4.target_ref
  0.7 0.0 copy-start
  0.7 1.4 %copy-done = f32[100,2,16,128]{3,2,1,0:T(8,128)S(1)} copy-done((f32[100,2,16,128]{3,2,1,0:T(8,128)S(1)}, f32[100,2,16,128]{3,2,1,0:T(8,128)}, u32[]{:S(2)}) %copy-start) | copy-done | bytes 1638424
  2.2 0.0 copy-start.1
  2.2 0.8 copy-done.1
  2.9 0.0 copy-start.2
  2.9 0.7 copy-done.2
  3.6 74.9 %shard_map.46 = f32[3200,128]{1,0:T(8,128)S(1)} custom-call(f32[3200,128]{1,0:T(8,128)S(1)} %bitcast.7, s32[64,128]{1,0:T(8,128)S(1)} %bitcast.8, f32[32,128]{1,0:T(8,128)S(1)} %pad.4.target_ref, s32[16]{0:T(128)S(1)} %copy-done.2), custom_call_target="tpu_custom_call" | custom-call | tf_op jit(solution)/shard_map/pallas_call | solution.py:288
  78.5 1.2 %copy.6 = f32[100,2,16,128]{3,2,1,0:T(8,128)} copy(f32[100,2,16,128]{3,2,1,0:T(8,128)S(1)} %bitcast.6) | data formatting | bytes 3276800
Async XLA Ops:
  0.7 1.4 %copy-start = (f32[100,2,16,128]{3,2,1,0:T(8,128)S(1)}, f32[100,2,16,128]{3,2,1,0:T(8,128)}, u32[]{:S(2)}) copy-start(f32[100,2,16,128]{3,2,1,0:T(8,128)} %param.4) | copy-start | bytes 4915204
  2.2 0.8 copy-start.1
  2.9 0.7 copy-start.2

commit v2 on v1

v2 whole, which is shorter than its diff:
```python
import functools

import jax
import jax.numpy as jnp
from jax import lax
from jax.experimental import pallas as pl
from jax.experimental.pallas import tpu as pltpu
from jax.sharding import PartitionSpec as P

LON_TAPS = (-0.0546875, 0.8203125, 0.2734375, -0.0390625)
LAT_TAPS = (-0.0625, 0.5625, 0.5625, -0.0625)
MESH = pl.DeviceIdType.MESH
F32 = jnp.float32
BF16 = jnp.bfloat16
TP = 112
KW = 384
BANDS = 24
ZGROUP = 4
CORES = 2
PITCH = 40
STEP = 4
CAP = 512
FLAG = 120


def tap_select(distance, taps):
    out = jnp.zeros(distance.shape, F32)
    for k in range(4):
        out = jnp.where(distance == k - 1, taps[k], out)
    return out


def lon_matrix(column, lcat, base):
    rows = lax.broadcasted_iota(jnp.int32, (128, 128), 0)
    main = tap_select(rows - column, LON_TAPS).astype(BF16)
    lcat[base:base + 128, :] = main
    lcat[base + 128:base + 256, :] = main
    e = lax.broadcasted_iota(jnp.int32, (16, 128), 0) % 8
    edge = jnp.where(e < 4, e - 4, e + 124)
    lcat[base + 256:base + 272, :] = tap_select(edge - column, LON_TAPS).astype(BF16)


def places(o1, direction):
    row = lax.broadcasted_iota(jnp.int32, (8, 128), 0)
    reach = lax.rem(row, 4) + o1
    need = reach >= 2 if direction else reach <= 0
    m = jnp.where(need, 1.0, 0.0)
    i = lax.broadcasted_iota(jnp.int32, (128, 128), 0)
    k = lax.broadcasted_iota(jnp.int32, (128, 128), 1)
    earlier = jnp.where(i < k, 1.0, 0.0).astype(BF16)
    m16 = jnp.concatenate([m, m], axis=0).astype(BF16)
    before = jnp.dot(m16, earlier, preferred_element_type=F32)[0:8]
    own = jnp.broadcast_to(jnp.sum(m, axis=1, keepdims=True), (8, 128))
    count = own
    for n in range(1, 8):
        above = jnp.where(row >= n, pltpu.roll(own, n, 0), 0.0)
        before = before + above
        count = count + above
    return jnp.where(need, before, -1.0).astype(jnp.int32), count


def kernel(dense, nt, nlat, nlon, x_hbm, off_hbm, target_hbm, mask_hbm, out_ref, flag_ref,
           xv, xb, offv, target_v, mask_v, es, er, ob, zs, zr, acc, lcat, sums, sums_t, ra, rb,
           pick, spread, fs, fr,
           local_sem, e_send, e_recv, o_send, o_recv, z_send, z_recv, a_send, a_recv, b_send, b_recv,
           f_send, f_recv):
    lat = lax.axis_index("lat")
    lon = lax.axis_index("lon")
    left = lax.rem(lon + nlon - 1, nlon)
    right = lax.rem(lon + 1, nlon)
    core = lax.rem(lon, CORES)
    zlo = lax.rem(lon // CORES, ZGROUP)
    ny = nlon // (ZGROUP * CORES)
    yy = lon // (ZGROUP * CORES)
    chunks = 8 if dense else CAP // 128

    load_x = pltpu.make_async_copy(
        x_hbm, xv.reshape(TP, PITCH, 128).at[pl.ds(0, nt), pl.ds(0, 32), :], local_sem.at[0])
    load_x.start()
    load_off = pltpu.make_async_copy(off_hbm, offv, local_sem.at[1])
    load_off.start()
    load_target = pltpu.make_async_copy(target_hbm, target_v, local_sem.at[2])
    load_target.start()
    load_mask = pltpu.make_async_copy(mask_hbm, mask_v, local_sem.at[3])
    load_mask.start()

    def z_peer(k):
        return {"lon": (yy * ZGROUP + lax.rem(zlo + k, ZGROUP)) * CORES + core}

    def y_peer(k):
        me = yy * CORES + core
        other = lax.rem(me + k, ny * CORES)
        return {"lon": ((other // CORES) * ZGROUP + zlo) * CORES + lax.rem(other, CORES)}

    def lat_peer(k):
        return {"lat": lax.rem(lat + k, nlat)}

    barrier = pltpu.get_barrier_semaphore()

    def greet(device):
        pl.semaphore_signal(barrier, inc=1, device_id=device, device_id_type=MESH)

    has_up = lat > 0
    has_down = lat < nlat - 1
    for k in range(1, nlat):
        greet(lat_peer(k))
    greet({"lon": left})
    greet({"lon": right})
    for k in range(1, ZGROUP):
        greet(z_peer(k))
    for k in range(1, ny * CORES):
        greet(y_peer(k))

    xv[pl.ds(nt * PITCH, (TP - nt) * PITCH), :] = jnp.zeros(((TP - nt) * PITCH, 128), F32)
    for l in range(2):
        for first in (0, 20):
            xb[pl.ds((l * BANDS + first) * TP, 4 * TP), :] = jnp.zeros((4 * TP, KW), BF16)
        lcat[l * KW + 272:(l + 1) * KW, :] = jnp.zeros((112, 128), BF16)
    lane = lax.broadcasted_iota(jnp.int32, (TP, 128), 1)

    load_off.wait()
    load_target.wait()
    load_mask.wait()
    load_x.wait()
    row = lax.rem(lax.broadcasted_iota(jnp.int32, (32, 128), 0), 16)
    mask = jnp.zeros((32, 128), F32)
    for j in range(16):
        mask = jnp.where(row == j, mask_v[j].astype(F32) * 0.5, mask)
    mask = mask[:, 0:nt]

    group = lane // 4

    def pack(step, carry):
        to_left, to_right = carry
        for i in range(STEP):
            lj = step * STEP + i
            v = xv[pl.ds(lj, TP, stride=PITCH), :]
            rolled = pltpu.roll(v, 4 * lj, 1)
            to_left = jnp.where(group == lj, rolled, to_left)
            to_right = jnp.where(group == lax.rem(lj + 31, 32), rolled, to_right)
            hi = v.astype(BF16)
            lo = (v - hi.astype(F32)).astype(BF16)
            row = pl.multiple_of(((lj // 16) * BANDS + 4 + lax.rem(lj, 16)) * TP, 16)
            xb[pl.ds(row, TP), 0:128] = hi
            xb[pl.ds(row, TP), 128:256] = lo
        return to_left, to_right

    zero = jnp.zeros((TP, 128), F32)
    with jax.named_scope("pack"):
        to_left, to_right = lax.fori_loop(0, 32 // STEP, pack, (zero, zero))
    es[0] = to_left
    es[1] = to_right

    with jax.named_scope("barw"):
        pl.semaphore_wait(barrier, (nlat - 1) + 2 + (ZGROUP - 1) + (ny * CORES - 1))

    ob4 = ob.reshape(2, 2, 2, 4, 128)

    def o_copy(direction):
        return pltpu.make_async_remote_copy(
            src_ref=offv.reshape(2, 2, 16, 128).at[:, :, pl.ds(12 * direction, 4), :],
            dst_ref=ob4.at[direction],
            send_sem=o_send.at[direction], recv_sem=o_recv.at[direction],
            device_id={"lat": lat - 1 + 2 * direction}, device_id_type=MESH)

    def e_copy(side):
        return pltpu.make_async_remote_copy(
            src_ref=es.at[side], dst_ref=er.at[1 - side],
            send_sem=e_send.at[side], recv_sem=e_recv.at[1 - side],
            device_id={"lon": left if side == 0 else right}, device_id_type=MESH)

    def z_copy(direction, s):
        return pltpu.make_async_remote_copy(
            src_ref=zs.at[direction, s, pl.ds(0, nt)], dst_ref=zr.at[direction, s, pl.ds(0, nt)],
            send_sem=z_send.at[direction, s], recv_sem=z_recv.at[direction, s],
            device_id={"lat": lat + 1 - 2 * direction}, device_id_type=MESH)

    @pl.when(has_up)
    def _():
        o_copy(0).start()

    @pl.when(has_down)
    def _():
        o_copy(1).start()

    e_copy(0).start()
    e_copy(1).start()

    f_copies = []
    place = []
    if not dense:
        flag = jnp.zeros((8, 128), F32)
        for direction in range(2):
            o1 = jnp.concatenate(
                [offv[pl.ds(32 + 12 * direction, 4), :], offv[pl.ds(48 + 12 * direction, 4), :]], axis=0)
            p, count = places(o1, direction)
            place.append(p)
            exists = has_up if direction == 0 else has_down
            flag = jnp.maximum(flag, jnp.where(count > CAP, exists.astype(F32), 0.0))
        fs[...] = jnp.broadcast_to(jnp.max(flag, axis=(0, 1), keepdims=True), (1, 128))
        for k in range(1, nlat):
            f_copies.append(pltpu.make_async_remote_copy(
                src_ref=fs, dst_ref=fr.at[k], send_sem=f_send.at[k], recv_sem=f_recv.at[k],
                device_id=lat_peer(k), device_id_type=MESH))
        for c in f_copies:
            c.start()

    with jax.named_scope("ewait"):
        for side in range(2):
            pltpu.make_async_remote_copy(
                src_ref=es.at[side], dst_ref=er.at[side], send_sem=e_send.at[side], recv_sem=e_recv.at[side],
                device_id={"lon": left}, device_id_type=MESH).wait_recv()

    def edges(first, step):
        for i in range(STEP):
            lj = 16 * (step // 2) + first + (4 if first else 12) * lax.rem(step, 2) + i
            shift = lax.rem(132 - 4 * lj, 128)
            a = pltpu.roll(er[0], shift, 1)
            b = pltpu.roll(er[1], shift, 1)
            e = jnp.where(lane < 4, a, b)
            hi = e.astype(BF16).astype(F32)
            both = jnp.where(lane < 8, hi, pltpu.roll(e - hi, 8, 1))
            row = pl.multiple_of(((lj // 16) * BANDS + 4 + lax.rem(lj, 16)) * TP, 16)
            xb[pl.ds(row, TP), 256:384] = both.astype(BF16)
        return 0

    with jax.named_scope("edges"):
        lax.fori_loop(0, 4, lambda step, _: edges(0, step), 0)

    def send_dense(direction):
        def part(s, _):
            l, jj = s // 4, lax.rem(s, 4)
            o0 = ob[pl.ds(16 * direction + s, 1), :]
            o1 = ob[pl.ds(16 * direction + 8 + s, 1), :]
            lon_matrix(o0 + lane[0:1], lcat, 0)
            start = pl.multiple_of((l * BANDS + 4 + 12 * (1 - direction)) * TP, 16)
            y = jnp.dot(xb[pl.ds(start, 4 * TP), :], lcat[0:KW, :], preferred_element_type=F32)
            total = jnp.zeros((TP, 128), F32)
            for hh in range(4):
                w = tap_select(hh + (4 if direction else -4) - jj - o1, LAT_TAPS)
                total = total + w * y[hh * TP:(hh + 1) * TP]
            zs[direction, s] = total
            z_copy(direction, s).start()
            return 0

        lax.fori_loop(0, 8, part, 0)

    def send_packed(direction):
        o0 = ob[pl.ds(16 * direction, 8), :]
        o1 = ob[pl.ds(16 * direction + 8, 8), :]
        row = lax.broadcasted_iota(jnp.int32, (8, 128), 0)
        column = lax.broadcasted_iota(jnp.int32, (8, 128), 1) + o0
        reach = lax.rem(row, 4) + o1
        number, _ = places(o1, direction)
        number_t = jnp.transpose(jnp.concatenate([number, jnp.zeros((120, 128), jnp.int32)], axis=0))
        slot = lax.broadcasted_iota(jnp.int32, (128, CAP), 1)
        row16 = lax.broadcasted_iota(jnp.int32, (16, 128), 0)
        cells = []
        for s in range(8):
            pick[s * 128:(s + 1) * 128, :] = jnp.where(number_t[:, s:s + 1] == slot, 1.0, 0.0).astype(BF16)
            v = jnp.where(row16 == 0, column[s:s + 1], jnp.where(row16 == 1, reach[s:s + 1], s // 4))
            cells.append(v.astype(F32).astype(BF16))
        known = jnp.dot(jnp.concatenate(cells, axis=1), pick[...], preferred_element_type=F32).astype(jnp.int32)
        for c in range(CAP // 128):
            column = known[0:1, c * 128:(c + 1) * 128]
            reach = known[1:2, c * 128:(c + 1) * 128]
            level = known[2:3, c * 128:(c + 1) * 128]
            y = jnp.zeros((4 * TP, 128), F32)
            for l in range(2):
                lon_matrix(jnp.where(level == l, column, 4096), lcat, l * KW)
                start = (l * BANDS + 4 + 12 * (1 - direction)) * TP
                y = y + jnp.dot(xb[start:start + 4 * TP, :], lcat[l * KW:(l + 1) * KW, :], preferred_element_type=F32)
            total = jnp.zeros((TP, 128), F32)
            for hh in range(4):
                w = tap_select(hh + (4 if direction else -4) - reach, LAT_TAPS)
                total = total + w * y[hh * TP:(hh + 1) * TP]
            zs[direction, c] = total
            z_copy(direction, c).start()

    for direction in range(2):
        @pl.when(has_up if direction else has_down)
        def _():
            with jax.named_scope("owait"):
                pltpu.make_async_remote_copy(
                    src_ref=ob4.at[direction], dst_ref=ob4.at[direction],
                    send_sem=o_send.at[direction], recv_sem=o_recv.at[direction],
                    device_id={"lat": lat + 1 - 2 * direction}, device_id_type=MESH).wait_recv()
            with jax.named_scope("part"):
                if dense:
                    send_dense(direction)
                else:
                    send_packed(direction)

    if not dense:
        slot = lax.broadcasted_iota(jnp.int32, (CAP, 128), 0)
        with jax.named_scope("spread"):
            for direction in range(2):
                for s in range(8):
                    spread[direction, :, s * 128:(s + 1) * 128] = jnp.where(
                        place[direction][s:s + 1] == slot, 1.0, 0.0).astype(BF16)

    with jax.named_scope("edges2"):
        lax.fori_loop(0, 4, lambda step, _: edges(4, step), 0)

    def own(lj, _):
        l, j = lj // 16, lax.rem(lj, 16)
        o0 = offv[pl.ds(lj, 1), :]
        o1 = offv[pl.ds(32 + lj, 1), :]
        lon_matrix(o0 + lane[0:1], lcat, 0)
        start = pl.multiple_of((l * BANDS + j) * TP, 16)
        y = jnp.dot(xb[pl.ds(start, 9 * TP), :], lcat[0:KW, :], preferred_element_type=F32)
        total = jnp.zeros((TP, 128), F32)
        for rr in range(9):
            w = tap_select(rr - 4 - o1, LAT_TAPS)
            total = total + w * y[rr * TP:(rr + 1) * TP]
        acc[lj] = total
        return 0

    with jax.named_scope("own"):
        lax.fori_loop(0, 32, own, 0)

    def square(first, step, total):
        for i in range(STEP):
            lj = 16 * (step // 2) + first + (4 if first else 12) * lax.rem(step, 2) + i
            a = acc[lj]
            total = jnp.where(lane == lj, jnp.sum(a * a, axis=1, keepdims=True), total)
        return total

    with jax.named_scope("square1"):
        total = lax.fori_loop(0, 4, lambda step, t: square(4, step, t), zero)

    for direction in range(2):
        def add(s, _):
            z_copy(direction, s).wait_recv()
            lj = (s // 4) * 16 + 12 * direction + lax.rem(s, 4)
            acc[lj] = acc[lj] + zr[direction, s]
            return 0

        def add_packed(c, _):
            z_copy(direction, c).wait_recv()
            z = zr[direction, c]
            hi = z.astype(BF16)
            both = jnp.concatenate([hi, (z - hi.astype(F32)).astype(BF16)], axis=0)
            start = pl.multiple_of(c * 128, 128)
            d = jnp.dot(both, spread[direction, pl.ds(start, 128), :], preferred_element_type=F32)
            for s in range(8):
                lj = (s // 4) * 16 + 12 * direction + s % 4
                acc[lj] = acc[lj] + (d[0:TP, s * 128:(s + 1) * 128] + d[TP:, s * 128:(s + 1) * 128])
            return 0

        @pl.when(has_down if direction else has_up)
        def _():
            with jax.named_scope("add"):
                lax.fori_loop(0, chunks, add if dense else add_packed, 0)

    with jax.named_scope("square2"):
        sums[0:TP, :] = lax.fori_loop(0, 4, lambda step, t: square(0, step, t), total)
    sums[TP:128, :] = jnp.zeros((128 - TP, 128), F32)
    row_sums = jnp.transpose(sums[...])[0:32]
    if not dense:
        flag = fs[...]
        for k, c in enumerate(f_copies):
            c.wait_recv()
            flag = flag + fr[k + 1]
        row_sums = jnp.where(lax.broadcasted_iota(jnp.int32, (32, 128), 1) >= FLAG, flag, row_sums)
    sums_t[...] = row_sums

    def exchange(peer, size, slots, send, recv, src):
        copies = []
        for k in range(1, size):
            copies.append(pltpu.make_async_remote_copy(
                src_ref=src, dst_ref=slots.at[k], send_sem=send.at[k], recv_sem=recv.at[k],
                device_id=peer(k), device_id_type=MESH))
        for c in copies:
            c.start()
        total = src[...]
        for k, c in enumerate(copies):
            c.wait_recv()
            total = total + slots[k + 1]
        return total, copies

    with jax.named_scope("exA"):
        total, a_copies = exchange(z_peer, ZGROUP, ra, a_send, a_recv, sums_t)
    ra[0] = total
    with jax.named_scope("exB"):
        total, b_copies = exchange(y_peer, ny * CORES, rb, b_send, b_recv, ra.at[0])
    flag_ref[...] = total[0:8]

    rms = jnp.sqrt(total * (1.0 / (128 * nlon)) + 1e-06)
    sums[0:32, 0:nt] = 1.0 + mask * (target_v[...] / rms[:, 0:nt] - 1.0)
    factor_t = jnp.transpose(sums[...])[0:TP]

    with jax.named_scope("scale"):
        for lj in range(32):
            out_ref[pl.ds(lj, nt, stride=32), :] = (acc[lj] * factor_t[:, lj:lj + 1])[0:nt]

    e_copy(0).wait_send()
    e_copy(1).wait_send()
    for c in a_copies + b_copies + f_copies:
        c.wait_send()
    for direction in range(2):
        @pl.when(has_up if direction else has_down)
        def _():
            o_copy(1 - direction).wait_send()
            lax.fori_loop(0, chunks, lambda s, _: (z_copy(direction, s).wait_send(), 0)[1], 0)


def solution(mesh):
    nlat, nlon = mesh.shape["lat"], mesh.shape["lon"]

    def body(tracers, offsets, target, band_mask):
        nt = tracers.shape[0]
        nb = nlon // ZGROUP
        vmem, dma = pltpu.VMEM, pltpu.SemaphoreType.DMA
        operands = (
            tracers.reshape(nt, 32, 128),
            offsets.reshape(64, 128),
            jnp.transpose(target, (1, 2, 0)).reshape(32, nt),
            band_mask,
        )

        def run(dense):
            return pl.pallas_call(
                functools.partial(kernel, dense, nt, nlat, nlon),
                out_shape=[jax.ShapeDtypeStruct((nt * 32, 128), F32), jax.ShapeDtypeStruct((8, 128), F32)],
                in_specs=[pl.BlockSpec(memory_space=pltpu.HBM)] * 4,
                out_specs=[pl.BlockSpec(memory_space=pltpu.VMEM)] * 2,
                scratch_shapes=[
                    vmem((TP * PITCH, 128), F32),
                    vmem((2 * BANDS * TP, KW), BF16),
                    vmem((64, 128), jnp.int32),
                    vmem((32, nt), F32),
                    pltpu.SMEM((16,), jnp.int32),
                    vmem((2, TP, 128), F32),
                    vmem((2, TP, 128), F32),
                    vmem((32, 128), jnp.int32),
                    vmem((2, 8, TP, 128), F32),
                    vmem((2, 8, TP, 128), F32),
                    vmem((32, TP, 128), F32),
                    vmem((2 * KW, 128), BF16),
                    vmem((128, 128), F32),
                    vmem((32, 128), F32),
                    vmem((ZGROUP, 32, 128), F32),
                    vmem((nb, 32, 128), F32),
                    vmem((1024, CAP), BF16),
                    vmem((2, CAP, 1024), BF16),
                    vmem((1, 128), F32),
                    vmem((nlat, 1, 128), F32),
                    dma((4,)), dma((2,)), dma((2,)), dma((2,)), dma((2,)), dma((2, 8)), dma((2, 8)),
                    dma((ZGROUP,)), dma((ZGROUP,)), dma((nb,)), dma((nb,)), dma((nlat,)), dma((nlat,)),
                ],
                compiler_params=pltpu.CompilerParams(
                    collective_id=int(dense), has_side_effects=True, vmem_limit_bytes=67043328
                ),
            )(*operands)

        out, flag = run(False)
        out = lax.cond(flag[0, FLAG] > 0.0, lambda: run(True)[0], lambda: out)
        return out.reshape(tracers.shape)

    placed = (
        P(None, None, "lat", "lon"),
        P(None, None, "lat", "lon"),
        P(None, None, "lat"),
        P("lat"),
    )
    return jax.shard_map(
        body, mesh=mesh, in_specs=placed, out_specs=P(None, None, "lat", "lon"), check_vma=False
    )
```

time: 79.9 us -> 55 us (0.69)
  Pallas kernels: 74.9 us -> 49.4 us
    pallas_call x1, Pallas kernels: 74.9 us -> 49.4 us  [run(): pl.pallas_call(functools.partial(kernel, dense, nt, nlat, nlon), out_shap...]
    unnamed x7 -> x1, local copies, waits for them, and re-layouts: 4.01 us -> 2.72 us
    slice x0 -> x1, local copies, waits for them, and re-layouts: none -> 1.26 us  [body(): out = lax.cond(flag[0, FLAG] > 0.0, lambda: run(True)[0], lambda: out)]
where the time goes in v2:
time: 55 us; the launch traced here: 54.1 us
  Pallas kernels  49.4 us (90%)
  local copies, waits for them, and re-layouts  3.98 us (7%)
  between operations  0.67 us (1%)
    pallas_call x1, Pallas kernels, run(): pl.pallas_call(functools.partial(kernel, dense, nt, nlat, nlon), out_shap...  49.4 us
    unnamed x1, local copies, waits for them, and re-layouts  2.72 us
    slice x1, local copies, waits for them, and re-layouts, body(): out = lax.cond(flag[0, FLAG] > 0.0, lambda: run(True)[0], lambda: out)  1.26 us

profile of v2, /device:TPU:1, one launch (start us, length us, event | category | flops | bytes accessed | tf_op | source)
XLA Modules:
  0.0 54.1 jit_solution(8010335322744834651)
XLA Ops:
  0.0 49.4 %shard_map.48 = (f32[3200,128]{1,0:T(8,128)}, f32[8,128]{1,0:T(8,128)}) custom-call(f32[100,32,128]{2,1,0:T(8,128)} %bitcast.8, s32[64,128]{1,0:T(8,128)} %bitcast.12, f32[32,100]{1,0:T(8,128)} %bitcast.14, s32[16]{0:T(128)} %mask_hbm.1), custom_call_target="tpu_custom_call" | custom-call | tf_op jit(solution)/shard_map/pallas_call | solution.py:423
  49.4 1.3 %slice.3 = f32[1,1]{1,0:T(1,128)} slice(f32[8,128]{1,0:T(8,128)} %get-tuple-element.26), slice={[0:1], [120:121]} | slice | bytes 8 | tf_op jit(solution)/shard_map/slice | solution.py:458
  51.3 2.7 %copy.11 = f32[100,2,16,128]{3,2,1,0:T(8,128)} copy(f32[100,2,16,128]{3,2,1,0:T(8,128)} %get-tuple-element.28) | data formatting | bytes 3276800
  (1 shorter events, 0.0 us)

commit v3 on v2

v3 whole, which is shorter than its diff:
```python
import functools

import jax
import jax.numpy as jnp
from jax import lax
from jax.experimental import pallas as pl
from jax.experimental.pallas import tpu as pltpu
from jax.sharding import PartitionSpec as P

LON_TAPS = (-0.0546875, 0.8203125, 0.2734375, -0.0390625)
LAT_TAPS = (-0.0625, 0.5625, 0.5625, -0.0625)
MESH = pl.DeviceIdType.MESH
F32 = jnp.float32
BF16 = jnp.bfloat16
TP = 112
KW = 384
BANDS = 24
ZGROUP = 4
CORES = 2
PITCH = 40
STEP = 4
CAP = 512
BLOCK = 25
FLAG = 120


def tap_select(distance, taps):
    out = jnp.zeros(distance.shape, F32)
    for k in range(4):
        out = jnp.where(distance == k - 1, taps[k], out)
    return out


def lon_matrix(column, lcat, base, lanes=slice(0, 128), edges=True):
    rows = lax.broadcasted_iota(jnp.int32, (128, 128), 0)
    main = tap_select(rows - column, LON_TAPS).astype(BF16)
    lcat[base:base + 128, lanes] = main
    lcat[base + 128:base + 256, lanes] = main
    if edges:
        e = lax.broadcasted_iota(jnp.int32, (16, 128), 0) % 8
        edge = jnp.where(e < 4, e - 4, e + 124)
        lcat[base + 256:base + 272, lanes] = tap_select(edge - column, LON_TAPS).astype(BF16)


def places(o0, o1, direction):
    row = lax.broadcasted_iota(jnp.int32, (8, 128), 0)
    column = lax.broadcasted_iota(jnp.int32, (8, 128), 1) + o0
    reach = lax.rem(row, 4) + o1
    need = jnp.where(reach >= 2 if direction else reach <= 0, 1.0, 0.0)
    edge = jnp.where(column <= 0, need, 0.0) + jnp.where(column >= 126, need, 0.0)
    i = lax.broadcasted_iota(jnp.int32, (128, 128), 0)
    k = lax.broadcasted_iota(jnp.int32, (128, 128), 1)
    earlier = jnp.where(i < k, 1.0, 0.0).astype(BF16)
    both = jnp.concatenate([need - edge, edge], axis=0)
    before = jnp.dot(both.astype(BF16), earlier, preferred_element_type=F32)
    own = jnp.broadcast_to(jnp.sum(both, axis=1, keepdims=True), (16, 128))
    inner, outer, count = before[0:8], before[8:16], own[0:8] + own[8:16]
    for n in range(1, 8):
        a = jnp.where(row >= n, pltpu.roll(own[0:8], n, 0), 0.0)
        b = jnp.where(row >= n, pltpu.roll(own[8:16], n, 0), 0.0)
        inner, outer, count = inner + a, outer + b, count + (a + b)
    number = jnp.where(need > 0.0, jnp.where(edge > 0.0, CAP - 1.0 - outer, inner), -1.0)
    return number.astype(jnp.int32), count


def kernel(dense, nt, nlat, nlon, x_hbm, off_hbm, target_hbm, mask_hbm, adv_hbm, fac_hbm, flag_hbm,
           xv, xb, offv, target_v, mask_v, es, er, ob, zs, zr, acc, lcat, lpair, sums, factor, flag_v, ra, rb,
           known, pick, spread, fs, fr,
           local_sem, e_send, e_recv, o_send, o_recv, z_send, z_recv, a_send, a_recv, b_send, b_recv,
           f_send, f_recv, w_sem):
    lat = lax.axis_index("lat")
    lon = lax.axis_index("lon")
    left = lax.rem(lon + nlon - 1, nlon)
    right = lax.rem(lon + 1, nlon)
    core = lax.rem(lon, CORES)
    zlo = lax.rem(lon // CORES, ZGROUP)
    ny = nlon // (ZGROUP * CORES)
    yy = lon // (ZGROUP * CORES)
    chunks = 8 if dense else CAP // 128

    load_x = pltpu.make_async_copy(
        x_hbm, xv.reshape(TP, PITCH, 128).at[pl.ds(0, nt), pl.ds(0, 32), :], local_sem.at[0])
    load_x.start()
    load_off = pltpu.make_async_copy(off_hbm, offv, local_sem.at[1])
    load_off.start()
    load_target = pltpu.make_async_copy(target_hbm, target_v, local_sem.at[2])
    load_target.start()
    load_mask = pltpu.make_async_copy(mask_hbm, mask_v, local_sem.at[3])
    load_mask.start()

    def z_peer(k):
        return {"lon": (yy * ZGROUP + lax.rem(zlo + k, ZGROUP)) * CORES + core}

    def y_peer(k):
        me = yy * CORES + core
        other = lax.rem(me + k, ny * CORES)
        return {"lon": ((other // CORES) * ZGROUP + zlo) * CORES + lax.rem(other, CORES)}

    def x_peer(k):
        return {"lat": lax.rem(lat + 2 * k, nlat)}

    barrier = pltpu.get_barrier_semaphore()

    def greet(device):
        pl.semaphore_signal(barrier, inc=1, device_id=device, device_id_type=MESH)

    has_up = lat > 0
    has_down = lat < nlat - 1

    @pl.when(has_up)
    def _():
        greet({"lat": lat - 1})

    @pl.when(has_down)
    def _():
        greet({"lat": lat + 1})

    for k in range(1, nlat // 2):
        greet(x_peer(k))
    greet({"lon": left})
    greet({"lon": right})
    for k in range(1, ZGROUP):
        greet(z_peer(k))
    for k in range(1, ny * CORES):
        greet(y_peer(k))

    xv[pl.ds(nt * PITCH, (TP - nt) * PITCH), :] = jnp.zeros(((TP - nt) * PITCH, 128), F32)
    for l in range(2):
        for first in (0, 20):
            xb[pl.ds((l * BANDS + first) * TP, 4 * TP), :] = jnp.zeros((4 * TP, KW), BF16)
        lcat[l * KW + 272:(l + 1) * KW, :] = jnp.zeros((112, 128), BF16)
    lpair[272:KW, :] = jnp.zeros((112, 256), BF16)
    lane = lax.broadcasted_iota(jnp.int32, (TP, 128), 1)

    load_off.wait()
    with jax.named_scope("barw"):
        pl.semaphore_wait(
            barrier,
            has_up.astype(jnp.int32) + has_down.astype(jnp.int32) + nlat // 2 + 1 + (ZGROUP - 1) + (ny * CORES - 1))

    ob4 = ob.reshape(2, 2, 2, 4, 128)

    def o_copy(direction):
        return pltpu.make_async_remote_copy(
            src_ref=offv.reshape(2, 2, 16, 128).at[:, :, pl.ds(12 * direction, 4), :],
            dst_ref=ob4.at[direction],
            send_sem=o_send.at[direction], recv_sem=o_recv.at[direction],
            device_id={"lat": lat - 1 + 2 * direction}, device_id_type=MESH)

    @pl.when(has_up)
    def _():
        o_copy(0).start()

    @pl.when(has_down)
    def _():
        o_copy(1).start()

    load_x.wait()

    group = lane // 4

    def pack(step, carry):
        to_left, to_right = carry
        for i in range(STEP):
            lj = step * STEP + i
            v = xv[pl.ds(lj, TP, stride=PITCH), :]
            rolled = pltpu.roll(v, 4 * lj, 1)
            to_left = jnp.where(group == lj, rolled, to_left)
            to_right = jnp.where(group == lax.rem(lj + 31, 32), rolled, to_right)
            hi = v.astype(BF16)
            lo = (v - hi.astype(F32)).astype(BF16)
            row = pl.multiple_of(((lj // 16) * BANDS + 4 + lax.rem(lj, 16)) * TP, 16)
            xb[pl.ds(row, TP), 0:128] = hi
            xb[pl.ds(row, TP), 128:256] = lo
        return to_left, to_right

    zero = jnp.zeros((TP, 128), F32)
    with jax.named_scope("pack"):
        to_left, to_right = lax.fori_loop(0, 32 // STEP, pack, (zero, zero))
    es[0] = to_left
    es[1] = to_right

    def e_copy(side):
        return pltpu.make_async_remote_copy(
            src_ref=es.at[side], dst_ref=er.at[1 - side],
            send_sem=e_send.at[side], recv_sem=e_recv.at[1 - side],
            device_id={"lon": left if side == 0 else right}, device_id_type=MESH)

    def z_copy(direction, s):
        return pltpu.make_async_remote_copy(
            src_ref=zs.at[direction, s, pl.ds(0, nt)], dst_ref=zr.at[direction, s, pl.ds(0, nt)],
            send_sem=z_send.at[direction, s], recv_sem=z_recv.at[direction, s],
            device_id={"lat": lat + 1 - 2 * direction}, device_id_type=MESH)

    e_copy(0).start()
    e_copy(1).start()

    f_copies = []
    place = []
    if not dense:
        flag = jnp.zeros((8, 128), F32)
        for direction in range(2):
            o0, o1 = [
                jnp.concatenate([offv[pl.ds(first + 12 * direction, 4), :], offv[pl.ds(first + 16 + 12 * direction, 4), :]], axis=0)
                for first in (0, 32)
            ]
            p, count = places(o0, o1, direction)
            place.append(p)
            exists = has_up if direction == 0 else has_down
            flag = jnp.maximum(flag, jnp.where(count > CAP, exists.astype(F32), 0.0))
        fs[0] = jnp.broadcast_to(jnp.max(flag, axis=(0, 1), keepdims=True), (1, 128))
        for k in range(nlat // 2):
            f_copies.append(pltpu.make_async_remote_copy(
                src_ref=fs.at[min(k, 1)], dst_ref=fr.at[k], send_sem=f_send.at[k], recv_sem=f_recv.at[k],
                device_id=x_peer(k) if k else {"lat": lat + 1 - 2 * lax.rem(lat, 2)}, device_id_type=MESH))
        f_copies[0].start()

    def edges(first, step):
        for i in range(STEP):
            lj = 16 * (step // 2) + first + (4 if first else 12) * lax.rem(step, 2) + i
            shift = lax.rem(132 - 4 * lj, 128)
            a = pltpu.roll(er[0], shift, 1)
            b = pltpu.roll(er[1], shift, 1)
            e = jnp.where(lane < 4, a, b)
            hi = e.astype(BF16).astype(F32)
            both = jnp.where(lane < 8, hi, pltpu.roll(e - hi, 8, 1))
            row = pl.multiple_of(((lj // 16) * BANDS + 4 + lax.rem(lj, 16)) * TP, 16)
            xb[pl.ds(row, TP), 256:384] = both.astype(BF16)
        return 0

    def send_dense(direction):
        def part(s, _):
            l, jj = s // 4, lax.rem(s, 4)
            o0 = ob[pl.ds(16 * direction + s, 1), :]
            o1 = ob[pl.ds(16 * direction + 8 + s, 1), :]
            lon_matrix(o0 + lane[0:1], lcat, 0)
            start = pl.multiple_of((l * BANDS + 4 + 12 * (1 - direction)) * TP, 16)
            y = jnp.dot(xb[pl.ds(start, 4 * TP), :], lcat[0:KW, :], preferred_element_type=F32)
            total = jnp.zeros((TP, 128), F32)
            for hh in range(4):
                w = tap_select(hh + (4 if direction else -4) - jj - o1, LAT_TAPS)
                total = total + w * y[hh * TP:(hh + 1) * TP]
            zs[direction, s] = total
            z_copy(direction, s).start()
            return 0

        lax.fori_loop(0, 8, part, 0)

    def find_cells(direction):
        o0 = ob[pl.ds(16 * direction, 8), :]
        o1 = ob[pl.ds(16 * direction + 8, 8), :]
        row = lax.broadcasted_iota(jnp.int32, (8, 128), 0)
        column = lax.broadcasted_iota(jnp.int32, (8, 128), 1) + o0
        reach = lax.rem(row, 4) + o1
        number, _ = places(o0, o1, direction)
        number_t = jnp.transpose(jnp.concatenate([number, jnp.zeros((120, 128), jnp.int32)], axis=0))
        slot = lax.broadcasted_iota(jnp.int32, (128, CAP), 1)
        row16 = lax.broadcasted_iota(jnp.int32, (16, 128), 0)
        cells = []
        for s in range(8):
            pick[s * 128:(s + 1) * 128, :] = jnp.where(number_t[:, s:s + 1] == slot, 1.0, 0.0).astype(BF16)
            v = jnp.where(row16 == 0, column[s:s + 1], jnp.where(row16 == 1, reach[s:s + 1], s // 4))
            cells.append(v.astype(F32).astype(BF16))
        found = jnp.dot(jnp.concatenate(cells, axis=1), pick[...], preferred_element_type=F32)
        known[direction] = found.astype(jnp.int32)

    def send_packed(direction, c, with_edges):
        here = slice(c * 128, (c + 1) * 128)
        column, reach, level = [known[direction, k:k + 1, here] for k in range(3)]
        depth = KW if with_edges else 256
        y = jnp.zeros((4 * TP, 128), F32)
        for l in range(2):
            lon_matrix(jnp.where(level == l, column, 4096), lcat, l * KW, edges=with_edges)
            start = (l * BANDS + 4 + 12 * (1 - direction)) * TP
            y = y + jnp.dot(
                xb[start:start + 4 * TP, 0:depth], lcat[l * KW:l * KW + depth, :], preferred_element_type=F32)
        total = jnp.zeros((TP, 128), F32)
        for hh in range(4):
            w = tap_select(hh + (4 if direction else -4) - reach, LAT_TAPS)
            total = total + w * y[hh * TP:(hh + 1) * TP]
        zs[direction, c] = total
        z_copy(direction, c).start()

    if dense:
        with jax.named_scope("ewait"):
            for side in range(2):
                pltpu.make_async_remote_copy(
                    src_ref=es.at[side], dst_ref=er.at[side], send_sem=e_send.at[side], recv_sem=e_recv.at[side],
                    device_id={"lon": left}, device_id_type=MESH).wait_recv()

        with jax.named_scope("edges"):
            lax.fori_loop(0, 4, lambda step, _: edges(0, step), 0)

    for direction in range(2):
        @pl.when(has_up if direction else has_down)
        def _():
            with jax.named_scope("owait"):
                pltpu.make_async_remote_copy(
                    src_ref=ob4.at[direction], dst_ref=ob4.at[direction],
                    send_sem=o_send.at[direction], recv_sem=o_recv.at[direction],
                    device_id={"lat": lat + 1 - 2 * direction}, device_id_type=MESH).wait_recv()
            with jax.named_scope("part"):
                if dense:
                    send_dense(direction)
                else:
                    find_cells(direction)
                    for c in range(CAP // 128 - 1):
                        send_packed(direction, c, False)

    if not dense:
        with jax.named_scope("ewait"):
            for side in range(2):
                pltpu.make_async_remote_copy(
                    src_ref=es.at[side], dst_ref=er.at[side], send_sem=e_send.at[side], recv_sem=e_recv.at[side],
                    device_id={"lon": left}, device_id_type=MESH).wait_recv()

        with jax.named_scope("edges"):
            lax.fori_loop(0, 4, lambda step, _: edges(0, step), 0)

        for direction in range(2):
            @pl.when(has_up if direction else has_down)
            def _():
                with jax.named_scope("part_edges"):
                    send_packed(direction, CAP // 128 - 1, True)

        slot = lax.broadcasted_iota(jnp.int32, (CAP, 128), 0)
        with jax.named_scope("spread"):
            for direction in range(2):
                for s in range(8):
                    spread[direction, :, s * 128:(s + 1) * 128] = jnp.where(
                        place[direction][s:s + 1] == slot, 1.0, 0.0).astype(BF16)

        f_copies[0].wait_recv()
        fs[1] = fs[0] + fr[0]
        for c in f_copies[1:]:
            c.start()

    with jax.named_scope("edges2"):
        lax.fori_loop(0, 4, lambda step, _: edges(4, step), 0)

    def own(pair, _):
        l, j = pair // 8, 2 * lax.rem(pair, 8)
        lj = 16 * l + j
        for i in range(2):
            lon_matrix(offv[pl.ds(lj + i, 1), :] + lane[0:1], lpair, 0, slice(128 * i, 128 * i + 128))
        start = pl.multiple_of((l * BANDS + j) * TP, 16)
        y = jnp.dot(xb[pl.ds(start, 10 * TP), :], lpair[...], preferred_element_type=F32)
        for i in range(2):
            o1 = offv[pl.ds(32 + lj + i, 1), :]
            total = jnp.zeros((TP, 128), F32)
            for rr in range(9):
                w = tap_select(rr - 4 - o1, LAT_TAPS)
                total = total + w * y[(rr + i) * TP:(rr + i + 1) * TP, 128 * i:128 * i + 128]
            acc[lj + i] = total
        return 0

    with jax.named_scope("own"):
        lax.fori_loop(0, 16, own, 0)

    def square(first, step, total):
        for i in range(STEP):
            a = acc[16 * (step // 2) + first + (4 if first else 12) * lax.rem(step, 2) + i]
            total = jnp.where(lane == 4 * step + i, jnp.sum(a * a, axis=1, keepdims=True), total)
        return total

    def row_sums(first):
        sums[0:TP, :] = lax.fori_loop(0, 4, lambda step, t: square(first, step, t), zero)
        sums[TP:128, :] = jnp.zeros((128 - TP, 128), F32)
        return jnp.transpose(sums[...])[0:16]

    def exchange(peer, size, slots, send, recv):
        return [
            pltpu.make_async_remote_copy(
                src_ref=slots.at[0], dst_ref=slots.at[k], send_sem=send.at[k], recv_sem=recv.at[k],
                device_id=peer(k), device_id_type=MESH)
            for k in range(1, size)
        ]

    def total_of(copies, slots):
        total = slots[0]
        for k, c in enumerate(copies):
            c.wait_recv()
            total = total + slots[k + 1]
        return total

    a_copies = [exchange(z_peer, ZGROUP, ra.at[n], a_send.at[n], a_recv.at[n]) for n in range(2)]
    b_copies = [exchange(y_peer, ny * CORES, rb.at[n], b_send.at[n], b_recv.at[n]) for n in range(2)]

    with jax.named_scope("square1"):
        inner = row_sums(4)
    if not dense:
        flag = fs[1]
        for k, c in enumerate(f_copies[1:]):
            c.wait_recv()
            flag = flag + fr[k + 1]
        inner = jnp.where(lax.broadcasted_iota(jnp.int32, (16, 128), 1) >= FLAG, flag, inner)
    ra[0, 0] = inner
    for c in a_copies[0]:
        c.start()

    def save(lj):
        return pltpu.make_async_copy(acc.at[lj, pl.ds(0, nt)], adv_hbm.at[:, lj], w_sem.at[lj])

    def save_rows(first):
        def one(k, _):
            save(16 * (k // 8) + (lax.rem(k, 8) + 4 if first else lax.rem(k, 8) + 8 * (lax.rem(k, 8) // 4))).start()
            return 0

        lax.fori_loop(0, 16, one, 0)

    save_rows(4)

    def add(direction, c):
        z_copy(direction, c).wait_recv()
        z = zr[direction, c]
        if dense:
            lj = (c // 4) * 16 + 12 * direction + lax.rem(c, 4)
            acc[lj] = acc[lj] + z
            return
        hi = z.astype(BF16)
        both = jnp.concatenate([hi, (z - hi.astype(F32)).astype(BF16)], axis=0)
        start = pl.multiple_of(c * 128, 128)
        d = jnp.dot(both, spread[direction, pl.ds(start, 128), :], preferred_element_type=F32)
        for s in range(8):
            lj = (s // 4) * 16 + 12 * direction + s % 4
            acc[lj] = acc[lj] + (d[0:TP, s * 128:(s + 1) * 128] + d[TP:, s * 128:(s + 1) * 128])

    def add_both(c, _):
        for direction in range(2):
            @pl.when(has_down if direction else has_up)
            def _():
                add(direction, c)
        return 0

    with jax.named_scope("add"):
        lax.fori_loop(0, chunks - 1, add_both, 0)
    with jax.named_scope("exA1"):
        rb[0, 0] = total_of(a_copies[0], ra.at[0])
        for c in b_copies[0]:
            c.start()
    with jax.named_scope("add_last"):
        add_both(chunks - 1, 0)

    with jax.named_scope("square2"):
        ra[1, 0] = row_sums(0)
    for c in a_copies[1]:
        c.start()
    save_rows(0)
    with jax.named_scope("exA"):
        rb[1, 0] = total_of(a_copies[1], ra.at[1])
    for c in b_copies[1]:
        c.start()
    with jax.named_scope("exB1"):
        inner = total_of(b_copies[0], rb.at[0])
    flag_v[0] = jnp.where(jnp.max(inner[0:8, FLAG:128]) > 0.0, 1, 0)
    put_flag = pltpu.make_async_copy(flag_v, flag_hbm, local_sem.at[0])
    put_flag.start()
    load_target.wait()
    load_mask.wait()
    row = lax.rem(lax.broadcasted_iota(jnp.int32, (32, 128), 0), 16)
    mask = jnp.zeros((32, 128), F32)
    for j in range(16):
        mask = jnp.where(row == j, mask_v[j].astype(F32) * 0.5, mask)
    with jax.named_scope("exB"):
        outer = total_of(b_copies[1], rb.at[1])
    for l in range(2):
        sums[16 * l:16 * l + 4, :] = outer[8 * l:8 * l + 4]
        sums[16 * l + 4:16 * l + 12, :] = inner[8 * l:8 * l + 8]
        sums[16 * l + 12:16 * l + 16, :] = outer[8 * l + 4:8 * l + 8]
    rms = jnp.sqrt(sums[0:32, :] * (1.0 / (128 * nlon)) + 1e-06)
    factor[:, 0:nt] = 1.0 + mask[:, 0:nt] * (target_v[...] / rms[:, 0:nt] - 1.0)
    put_factor = pltpu.make_async_copy(factor, fac_hbm, local_sem.at[1])
    put_factor.start()

    lax.fori_loop(0, 32, lambda lj, _: (save(lj).wait(), 0)[1], 0)
    e_copy(0).wait_send()
    e_copy(1).wait_send()
    for c in a_copies[0] + a_copies[1] + b_copies[0] + b_copies[1] + f_copies:
        c.wait_send()
    for direction in range(2):
        @pl.when(has_up if direction else has_down)
        def _():
            o_copy(1 - direction).wait_send()
            lax.fori_loop(0, chunks, lambda s, _: (z_copy(direction, s).wait_send(), 0)[1], 0)
    put_flag.wait()
    put_factor.wait()


def scale(fac_hbm, adv_hbm, out_hbm, fac_v, rows_v, in_sem, out_sem, fac_sem):
    size = BLOCK * 32
    parts = rows_v.shape[0]
    load_fac = pltpu.make_async_copy(fac_hbm, fac_v, fac_sem)
    load_fac.start()
    loads = [pltpu.make_async_copy(adv_hbm.at[pl.ds(size * n, size)], rows_v.at[n], in_sem.at[n]) for n in range(parts)]
    stores = [pltpu.make_async_copy(rows_v.at[n], out_hbm.at[pl.ds(size * n, size)], out_sem.at[n]) for n in range(parts)]
    for c in loads:
        c.start()
    load_fac.wait()
    for n in range(parts):
        loads[n].wait()
        for t in range(BLOCK):
            here = slice(32 * t, 32 * t + 32)
            column = BLOCK * n + t
            rows_v[n, here, :] = rows_v[n, here, :] * fac_v[:, column:column + 1]
        stores[n].start()
    for c in stores:
        c.wait()


def solution(mesh):
    nlat, nlon = mesh.shape["lat"], mesh.shape["lon"]

    def body(tracers, offsets, target, band_mask):
        nt = tracers.shape[0]
        nb = nlon // ZGROUP
        vmem, dma = pltpu.VMEM, pltpu.SemaphoreType.DMA
        operands = (
            tracers.reshape(nt, 32, 128),
            offsets.reshape(64, 128),
            jnp.transpose(target, (1, 2, 0)).reshape(32, nt),
            band_mask,
        )

        def run(dense):
            return pl.pallas_call(
                functools.partial(kernel, dense, nt, nlat, nlon),
                out_shape=[
                    jax.ShapeDtypeStruct((nt, 32, 128), F32),
                    jax.ShapeDtypeStruct((32, 128), F32),
                    jax.ShapeDtypeStruct((1,), jnp.int32),
                ],
                in_specs=[pl.BlockSpec(memory_space=pltpu.HBM)] * 4,
                out_specs=[pl.BlockSpec(memory_space=pltpu.HBM)] * 3,
                scratch_shapes=[
                    vmem((TP * PITCH, 128), F32),
                    vmem((2 * BANDS * TP, KW), BF16),
                    vmem((64, 128), jnp.int32),
                    vmem((32, nt), F32),
                    pltpu.SMEM((16,), jnp.int32),
                    vmem((2, TP, 128), F32),
                    vmem((2, TP, 128), F32),
                    vmem((32, 128), jnp.int32),
                    vmem((2, 8, TP, 128), F32),
                    vmem((2, 8, TP, 128), F32),
                    vmem((32, TP, 128), F32),
                    vmem((2 * KW, 128), BF16),
                    vmem((KW, 256), BF16),
                    vmem((128, 128), F32),
                    vmem((32, 128), F32),
                    pltpu.SMEM((1,), jnp.int32),
                    vmem((2, ZGROUP, 16, 128), F32),
                    vmem((2, nb, 16, 128), F32),
                    vmem((2, 16, CAP), jnp.int32),
                    vmem((1024, CAP), BF16),
                    vmem((2, CAP, 1024), BF16),
                    vmem((2, 1, 128), F32),
                    vmem((nlat // 2, 1, 128), F32),
                    dma((4,)), dma((2,)), dma((2,)), dma((2,)), dma((2,)), dma((2, 8)), dma((2, 8)),
                    dma((2, ZGROUP)), dma((2, ZGROUP)), dma((2, nb)), dma((2, nb)), dma((nlat // 2,)), dma((nlat // 2,)), dma((32,)),
                ],
                compiler_params=pltpu.CompilerParams(
                    collective_id=int(dense), has_side_effects=True, vmem_limit_bytes=67043328
                ),
            )(*operands)

        adv, fac, flag = run(False)
        adv, fac = lax.cond(flag[0] > 0, lambda: tuple(run(True)[0:2]), lambda: (adv, fac))
        out = pl.pallas_call(
            scale,
            out_shape=jax.ShapeDtypeStruct((nt * 32, 128), F32),
            in_specs=[pl.BlockSpec(memory_space=pltpu.HBM)] * 2,
            out_specs=pl.BlockSpec(memory_space=pltpu.HBM),
            scratch_shapes=[
                vmem((32, 128), F32), vmem((nt // BLOCK, BLOCK * 32, 128), F32), dma((nt // BLOCK,)), dma((nt // BLOCK,)), dma,
            ],
            compiler_params=pltpu.CompilerParams(vmem_limit_bytes=67043328),
        )(fac, adv.reshape(nt * 32, 128))
        return out.reshape(tracers.shape)

    placed = (
        P(None, None, "lat", "lon"),
        P(None, None, "lat", "lon"),
        P(None, None, "lat"),
        P("lat"),
    )
    return jax.shard_map(
        body, mesh=mesh, in_specs=placed, out_specs=P(None, None, "lat", "lon"), check_vma=False
    )
```

time: 55 us -> 50.2 us (0.913)
  local copies, waits for them, and re-layouts: 3.98 us -> 0 us
  Pallas kernels: 49.4 us -> 48.8 us
    pallas_call x1, Pallas kernels: 49.4 us -> 46.1 us  [run(): pl.pallas_call(functools.partial(kernel, dense, nt, nlat, nlon), out_shap...]
    pallas_call x0 -> x1, Pallas kernels: none -> 2.77 us  [body(): pl.pallas_call(scale, out_shape=jax.ShapeDtypeStruct((nt * 32, 128), F32)...]
    unnamed x1 -> x0, local copies, waits for them, and re-layouts: 2.72 us -> none
    slice x1 -> x0, local copies, waits for them, and re-layouts: 1.26 us -> none  [body(): out = lax.cond(flag[0, FLAG] > 0.0, lambda: run(True)[0], lambda: out)]
where the time goes in v3:
time: 50.2 us; the launch traced here: 49.5 us
  Pallas kernels  48.8 us (97%)
  between operations  0.69 us (1%)
    pallas_call x1, Pallas kernels, run(): pl.pallas_call(functools.partial(kernel, dense, nt, nlat, nlon), out_shap...  46.1 us
    pallas_call x1, Pallas kernels, body(): pl.pallas_call(scale, out_shape=jax.ShapeDtypeStruct((nt * 32, 128), F32)...  2.77 us

profile of v3, /device:TPU:1, one launch (start us, length us, event | category | flops | bytes accessed | tf_op | source)
XLA Modules:
  0.0 49.5 jit_solution(5076497626825697970)
XLA Ops:
  0.0 46.1 %shard_map.46 = (f32[100,32,128]{2,1,0:T(8,128)}, f32[32,128]{1,0:T(8,128)}, s32[1]{0:T(128)}) custom-call(f32[100,32,128]{2,1,0:T(8,128)} %bitcast.8, s32[64,128]{1,0:T(8,128)} %bitcast.11, f32[32,100]{1,0:T(8,128)} %bitcast.13, s32[16]{0:T(128)} %mask_hbm.1), custom_call_target="tpu_custom_call" | custom-call | tf_op jit(solution)/shard_map/pallas_call | solution.py:525
  46.8 2.8 %shard_map.47 = f32[3200,128]{1,0:T(8,128)} custom-call(f32[32,128]{1,0:T(8,128)} %get-tuple-element.41.fac_hbm, f32[3200,128]{1,0:T(8,128)} %bitcast.10), custom_call_target="tpu_custom_call" | custom-call | tf_op jit(solution)/shard_map/pallas_call | solution.py:568
  (1 shorter events, 0.0 us)

commit v4 on v3

--- a/solution.py
+++ b/solution.py
@@ -20,7 +20,6 @@
 PITCH = 40
 STEP = 4
 CAP = 512
-BLOCK = 25
 FLAG = 120
 
 
@@ -63,11 +62,11 @@
     return number.astype(jnp.int32), count
 
 
-def kernel(dense, nt, nlat, nlon, x_hbm, off_hbm, target_hbm, mask_hbm, adv_hbm, fac_hbm, flag_hbm,
-           xv, xb, offv, target_v, mask_v, es, er, ob, zs, zr, acc, lcat, lpair, sums, factor, flag_v, ra, rb,
+def kernel(dense, nt, nlat, nlon, x_hbm, off_hbm, target_hbm, mask_hbm, out_ref, flag_hbm,
+           xv, xb, offv, target_v, mask_v, es, er, ob, zs, zr, acc, lcat, lpair, sums, flag_v, ra, rb,
            known, pick, spread, fs, fr,
            local_sem, e_send, e_recv, o_send, o_recv, z_send, z_recv, a_send, a_recv, b_send, b_recv,
-           f_send, f_recv, w_sem):
+           f_send, f_recv):
     lat = lax.axis_index("lat")
     lon = lax.axis_index("lon")
     left = lax.rem(lon + nlon - 1, nlon)
@@ -182,7 +181,7 @@
 
     def e_copy(side):
         return pltpu.make_async_remote_copy(
-            src_ref=es.at[side], dst_ref=er.at[1 - side],
+            src_ref=es.at[side, pl.ds(0, nt)], dst_ref=er.at[1 - side, pl.ds(0, nt)],
             send_sem=e_send.at[side], recv_sem=e_recv.at[1 - side],
             device_id={"lon": left if side == 0 else right}, device_id_type=MESH)
 
@@ -285,7 +284,7 @@
         with jax.named_scope("ewait"):
             for side in range(2):
                 pltpu.make_async_remote_copy(
-                    src_ref=es.at[side], dst_ref=er.at[side], send_sem=e_send.at[side], recv_sem=e_recv.at[side],
+                    src_ref=es.at[side, pl.ds(0, nt)], dst_ref=er.at[side, pl.ds(0, nt)], send_sem=e_send.at[side], recv_sem=e_recv.at[side],
                     device_id={"lon": left}, device_id_type=MESH).wait_recv()
 
         with jax.named_scope("edges"):
@@ -311,7 +310,7 @@
         with jax.named_scope("ewait"):
             for side in range(2):
                 pltpu.make_async_remote_copy(
-                    src_ref=es.at[side], dst_ref=er.at[side], send_sem=e_send.at[side], recv_sem=e_recv.at[side],
+                    src_ref=es.at[side, pl.ds(0, nt)], dst_ref=er.at[side, pl.ds(0, nt)], send_sem=e_send.at[side], recv_sem=e_recv.at[side],
                     device_id={"lon": left}, device_id_type=MESH).wait_recv()
 
         with jax.named_scope("edges"):
@@ -338,8 +337,9 @@
     with jax.named_scope("edges2"):
         lax.fori_loop(0, 4, lambda step, _: edges(4, step), 0)
 
-    def own(pair, _):
-        l, j = pair // 8, 2 * lax.rem(pair, 8)
+    def own(pair, inner):
+        q = lax.rem(pair, 4)
+        l, j = pair // 4, 2 * q + (4 if inner else 8 * (q // 2))
         lj = 16 * l + j
         for i in range(2):
             lon_matrix(offv[pl.ds(lj + i, 1), :] + lane[0:1], lpair, 0, slice(128 * i, 128 * i + 128))
@@ -354,17 +354,15 @@
             acc[lj + i] = total
         return 0
 
-    with jax.named_scope("own"):
-        lax.fori_loop(0, 16, own, 0)
-
-    def square(first, step, total):
-        for i in range(STEP):
-            a = acc[16 * (step // 2) + first + (4 if first else 12) * lax.rem(step, 2) + i]
-            total = jnp.where(lane == 4 * step + i, jnp.sum(a * a, axis=1, keepdims=True), total)
-        return total
+    with jax.named_scope("own_inner"):
+        lax.fori_loop(0, 8, lambda pair, _: own(pair, True), 0)
 
     def row_sums(first):
-        sums[0:TP, :] = lax.fori_loop(0, 4, lambda step, t: square(first, step, t), zero)
+        total = zero
+        for n in range(16):
+            a = acc[16 * (n // 8) + first + (n % 8 if first else n % 8 + 8 * (n % 8 // 4))]
+            total = jnp.where(lane == n, jnp.sum(a * a, axis=1, keepdims=True), total)
+        sums[0:TP, :] = total
         sums[TP:128, :] = jnp.zeros((128 - TP, 128), F32)
         return jnp.transpose(sums[...])[0:16]
 
@@ -398,17 +396,15 @@
     for c in a_copies[0]:
         c.start()
 
-    def save(lj):
-        return pltpu.make_async_copy(acc.at[lj, pl.ds(0, nt)], adv_hbm.at[:, lj], w_sem.at[lj])
-
     def save_rows(first):
-        def one(k, _):
-            save(16 * (k // 8) + (lax.rem(k, 8) + 4 if first else lax.rem(k, 8) + 8 * (lax.rem(k, 8) // 4))).start()
-            return 0
-
-        lax.fori_loop(0, 16, one, 0)
+        for n in range(16):
+            lj = 16 * (n // 8) + first + (n % 8 if first else n % 8 + 8 * (n % 8 // 4))
+            out_ref[pl.ds(lj, nt, stride=32), :] = acc[lj, 0:nt]
 
     save_rows(4)
+
+    with jax.named_scope("own_outer"):
+        lax.fori_loop(0, 8, lambda pair, _: own(pair, False), 0)
 
     def add(direction, c):
         z_copy(direction, c).wait_recv()
@@ -468,11 +464,12 @@
         sums[16 * l + 4:16 * l + 12, :] = inner[8 * l:8 * l + 8]
         sums[16 * l + 12:16 * l + 16, :] = outer[8 * l + 4:8 * l + 8]
     rms = jnp.sqrt(sums[0:32, :] * (1.0 / (128 * nlon)) + 1e-06)
-    factor[:, 0:nt] = 1.0 + mask[:, 0:nt] * (target_v[...] / rms[:, 0:nt] - 1.0)
-    put_factor = pltpu.make_async_copy(factor, fac_hbm, local_sem.at[1])
-    put_factor.start()
-
-    lax.fori_loop(0, 32, lambda lj, _: (save(lj).wait(), 0)[1], 0)
+    factor = 1.0 + mask[:, 0:nt] * (target_v[...] / rms[:, 0:nt] - 1.0)
+    with jax.named_scope("scale"):
+        for t in range(nt):
+            here = slice(32 * t, 32 * t + 32)
+            out_ref[here, :] = out_ref[here, :] * factor[:, t:t + 1]
+
     e_copy(0).wait_send()
     e_copy(1).wait_send()
     for c in a_copies[0] + a_copies[1] + b_copies[0] + b_copies[1] + f_copies:
@@ -483,28 +480,6 @@
             o_copy(1 - direction).wait_send()
             lax.fori_loop(0, chunks, lambda s, _: (z_copy(direction, s).wait_send(), 0)[1], 0)
     put_flag.wait()
-    put_factor.wait()
-
-
-def scale(fac_hbm, adv_hbm, out_hbm, fac_v, rows_v, in_sem, out_sem, fac_sem):
-    size = BLOCK * 32
-    parts = rows_v.shape[0]
-    load_fac = pltpu.make_async_copy(fac_hbm, fac_v, fac_sem)
-    load_fac.start()
-    loads = [pltpu.make_async_copy(adv_hbm.at[pl.ds(size * n, size)], rows_v.at[n], in_sem.at[n]) for n in range(parts)]
-    stores = [pltpu.make_async_copy(rows_v.at[n], out_hbm.at[pl.ds(size * n, size)], out_sem.at[n]) for n in range(parts)]
-    for c in loads:
-        c.start()
-    load_fac.wait()
-    for n in range(parts):
-        loads[n].wait()
-        for t in range(BLOCK):
-            here = slice(32 * t, 32 * t + 32)
-            column = BLOCK * n + t
-            rows_v[n, here, :] = rows_v[n, here, :] * fac_v[:, column:column + 1]
-        stores[n].start()
-    for c in stores:
-        c.wait()
 
 
 def solution(mesh):
@@ -514,23 +489,22 @@
         nt = tracers.shape[0]
         nb = nlon // ZGROUP
         vmem, dma = pltpu.VMEM, pltpu.SemaphoreType.DMA
-        operands = (
+        operands = tuple(pltpu.with_memory_space_constraint(a, pltpu.HBM) for a in (
             tracers.reshape(nt, 32, 128),
             offsets.reshape(64, 128),
             jnp.transpose(target, (1, 2, 0)).reshape(32, nt),
             band_mask,
-        )
+        ))
 
         def run(dense):
             return pl.pallas_call(
                 functools.partial(kernel, dense, nt, nlat, nlon),
                 out_shape=[
-                    jax.ShapeDtypeStruct((nt, 32, 128), F32),
-                    jax.ShapeDtypeStruct((32, 128), F32),
+                    jax.ShapeDtypeStruct((nt * 32, 128), F32),
                     jax.ShapeDtypeStruct((1,), jnp.int32),
                 ],
                 in_specs=[pl.BlockSpec(memory_space=pltpu.HBM)] * 4,
-                out_specs=[pl.BlockSpec(memory_space=pltpu.HBM)] * 3,
+                out_specs=[pl.BlockSpec(memory_space=pltpu.VMEM), pl.BlockSpec(memory_space=pltpu.HBM)],
                 scratch_shapes=[
                     vmem((TP * PITCH, 128), F32),
                     vmem((2 * BANDS * TP, KW), BF16),
@@ -546,7 +520,6 @@
                     vmem((2 * KW, 128), BF16),
                     vmem((KW, 256), BF16),
                     vmem((128, 128), F32),
-                    vmem((32, 128), F32),
                     pltpu.SMEM((1,), jnp.int32),
                     vmem((2, ZGROUP, 16, 128), F32),
                     vmem((2, nb, 16, 128), F32),
@@ -556,25 +529,15 @@
                     vmem((2, 1, 128), F32),
                     vmem((nlat // 2, 1, 128), F32),
                     dma((4,)), dma((2,)), dma((2,)), dma((2,)), dma((2,)), dma((2, 8)), dma((2, 8)),
-                    dma((2, ZGROUP)), dma((2, ZGROUP)), dma((2, nb)), dma((2, nb)), dma((nlat // 2,)), dma((nlat // 2,)), dma((32,)),
+                    dma((2, ZGROUP)), dma((2, ZGROUP)), dma((2, nb)), dma((2, nb)), dma((nlat // 2,)), dma((nlat // 2,)),
                 ],
                 compiler_params=pltpu.CompilerParams(
-                    collective_id=int(dense), has_side_effects=True, vmem_limit_bytes=67043328
+                    collective_id=int(dense), has_side_effects=True, vmem_limit_bytes=50000000
                 ),
             )(*operands)
 
-        adv, fac, flag = run(False)
-        adv, fac = lax.cond(flag[0] > 0, lambda: tuple(run(True)[0:2]), lambda: (adv, fac))
-        out = pl.pallas_call(
-            scale,
-            out_shape=jax.ShapeDtypeStruct((nt * 32, 128), F32),
-            in_specs=[pl.BlockSpec(memory_space=pltpu.HBM)] * 2,
-            out_specs=pl.BlockSpec(memory_space=pltpu.HBM),
-            scratch_shapes=[
-                vmem((32, 128), F32), vmem((nt // BLOCK, BLOCK * 32, 128), F32), dma((nt // BLOCK,)), dma((nt // BLOCK,)), dma,
-            ],
-            compiler_params=pltpu.CompilerParams(vmem_limit_bytes=67043328),
-        )(fac, adv.reshape(nt * 32, 128))
+        out, flag = run(False)
+        out = lax.cond(flag[0] > 0, lambda: run(True)[0], lambda: out)
         return out.reshape(tracers.shape)
 
     placed = (

time: 50.2 us -> 47.7 us (0.950); the launches traced: 49.5 us -> 47.6 us
  Pallas kernels: 48.8 us -> 45.8 us
  local copies, waits for them, and re-layouts: 0 us -> 1.17 us
    pallas_call x1 -> x0, Pallas kernels: 2.77 us -> none  [body(): pl.pallas_call(scale, out_shape=jax.ShapeDtypeStruct((nt * 32, 128), F32)...]
    unnamed x0 -> x1, local copies, waits for them, and re-layouts: none -> 1.17 us
where the time goes in v4:
time: 47.7 us; the launch traced here: 47.6 us
  Pallas kernels  45.8 us (96%)
  local copies, waits for them, and re-layouts  1.17 us (2%)
  between operations  0.63 us (1%)
    pallas_call x1, Pallas kernels, run(): pl.pallas_call(functools.partial(kernel, dense, nt, nlat, nlon), out_shap...  45.8 us
    unnamed x1, local copies, waits for them, and re-layouts  1.17 us

profile of v4, /device:TPU:1, one launch (start us, length us, event | category | flops | bytes accessed | tf_op | source)
XLA Modules:
  0.0 47.6 jit_solution(10787985464807972489)
XLA Ops:
  0.0 45.8 %shard_map.48 = (f32[3200,128]{1,0:T(8,128)S(1)}, s32[1]{0:T(128)}) custom-call(f32[100,32,128]{2,1,0:T(8,128)} %bitcast.8, s32[64,128]{1,0:T(8,128)} %bitcast.12, f32[32,100]{1,0:T(8,128)} %bitcast.14, s32[16]{0:T(128)} %mask_hbm.1), custom_call_target="tpu_custom_call" | custom-call | tf_op jit(solution)/shard_map/pallas_call | solution.py:500
  46.5 1.2 %copy.11 = f32[100,2,16,128]{3,2,1,0:T(8,128)} copy(f32[100,2,16,128]{3,2,1,0:T(8,128)S(1)} %get-tuple-element.28) | data formatting | bytes 3276800
  (1 shorter events, 0.0 us)

commit v5 on v4

--- a/solution.py
+++ b/solution.py
@@ -19,7 +19,9 @@
 CORES = 2
 PITCH = 40
 STEP = 4
-CAP = 512
+SLOTS = 512
+CAP = 416
+REST = 32
 FLAG = 120
 
 
@@ -41,16 +43,27 @@
         lcat[base + 256:base + 272, lanes] = tap_select(edge - column, LON_TAPS).astype(BF16)
 
 
-def places(o0, o1, direction):
+def border_cells(o0, o1, direction):
     row = lax.broadcasted_iota(jnp.int32, (8, 128), 0)
     column = lax.broadcasted_iota(jnp.int32, (8, 128), 1) + o0
     reach = lax.rem(row, 4) + o1
-    need = jnp.where(reach >= 2 if direction else reach <= 0, 1.0, 0.0)
-    edge = jnp.where(column <= 0, need, 0.0) + jnp.where(column >= 126, need, 0.0)
+    used = jnp.maximum(reach - 1 if direction else 1 - reach, 0)
+    inside = jnp.where(column <= 0, 0, jnp.where(column >= 126, 0, 1))
+    edge = jnp.where(used > 0, 1.0, 0.0) * jnp.where(inside > 0, 0.0, 1.0)
+    used = used * inside
+    shared = jnp.zeros((8, 128), F32)
+    for k in range(1, 5):
+        here = jnp.zeros((8, 128), F32)
+        for shift in range(-3, 3):
+            hit = jnp.where(o0 == shift, jnp.where(used == k, 1.0, 0.0), 0.0)
+            here = jnp.maximum(here, pltpu.roll(hit, shift % 128, 1) if shift else hit)
+        for l in range(2):
+            top = jnp.max(here[4 * l:4 * l + 4], axis=0, keepdims=True)
+            shared = jnp.where(row == 4 * l + k - 1, top, shared)
     i = lax.broadcasted_iota(jnp.int32, (128, 128), 0)
     k = lax.broadcasted_iota(jnp.int32, (128, 128), 1)
     earlier = jnp.where(i < k, 1.0, 0.0).astype(BF16)
-    both = jnp.concatenate([need - edge, edge], axis=0)
+    both = jnp.concatenate([shared, edge], axis=0)
     before = jnp.dot(both.astype(BF16), earlier, preferred_element_type=F32)
     own = jnp.broadcast_to(jnp.sum(both, axis=1, keepdims=True), (16, 128))
     inner, outer, count = before[0:8], before[8:16], own[0:8] + own[8:16]
@@ -58,13 +71,26 @@
         a = jnp.where(row >= n, pltpu.roll(own[0:8], n, 0), 0.0)
         b = jnp.where(row >= n, pltpu.roll(own[8:16], n, 0), 0.0)
         inner, outer, count = inner + a, outer + b, count + (a + b)
-    number = jnp.where(need > 0.0, jnp.where(edge > 0.0, CAP - 1.0 - outer, inner), -1.0)
+    inner = jnp.where(shared > 0.0, inner, -1.0)
+    outer = jnp.where(edge > 0.0, CAP - 1.0 - outer, -1.0)
+    return used, inner, outer, count
+
+
+def places(o0, o1, direction):
+    used, inner, outer, count = border_cells(o0, o1, direction)
+    row = lax.broadcasted_iota(jnp.int32, (8, 128), 0)
+    number = outer
+    for k in range(1, 5):
+        of_level = jnp.where(row < 4, inner[k - 1:k], inner[k + 3:k + 4])
+        for shift in range(-3, 3):
+            there = pltpu.roll(of_level, -shift % 128, 1) if shift else of_level
+            number = jnp.where(o0 == shift, jnp.where(used == k, there, number), number)
     return number.astype(jnp.int32), count
 
 
 def kernel(dense, nt, nlat, nlon, x_hbm, off_hbm, target_hbm, mask_hbm, out_ref, flag_hbm,
            xv, xb, offv, target_v, mask_v, es, er, ob, zs, zr, acc, lcat, lpair, sums, flag_v, ra, rb,
-           known, pick, spread, fs, fr,
+           numbers, known, pick, spread, fs, fr,
            local_sem, e_send, e_recv, o_send, o_recv, z_send, z_recv, a_send, a_recv, b_send, b_recv,
            f_send, f_recv):
     lat = lax.axis_index("lat")
@@ -75,7 +101,7 @@
     zlo = lax.rem(lon // CORES, ZGROUP)
     ny = nlon // (ZGROUP * CORES)
     yy = lon // (ZGROUP * CORES)
-    chunks = 8 if dense else CAP // 128
+    chunks = 8 if dense else SLOTS // 128
 
     load_x = pltpu.make_async_copy(
         x_hbm, xv.reshape(TP, PITCH, 128).at[pl.ds(0, nt), pl.ds(0, 32), :], local_sem.at[0])
@@ -185,9 +211,10 @@
             send_sem=e_send.at[side], recv_sem=e_recv.at[1 - side],
             device_id={"lon": left if side == 0 else right}, device_id_type=MESH)
 
-    def z_copy(direction, s):
+    def z_copy(direction, s, last=False):
+        rows = pl.ds(0, REST if last and not dense else nt)
         return pltpu.make_async_remote_copy(
-            src_ref=zs.at[direction, s, pl.ds(0, nt)], dst_ref=zr.at[direction, s, pl.ds(0, nt)],
+            src_ref=zs.at[direction, s, rows], dst_ref=zr.at[direction, s, rows],
             send_sem=z_send.at[direction, s], recv_sem=z_recv.at[direction, s],
             device_id={"lat": lat + 1 - 2 * direction}, device_id_type=MESH)
 
@@ -245,23 +272,34 @@
 
         lax.fori_loop(0, 8, part, 0)
 
-    def find_cells(direction):
+    def find_cells(direction, edge):
         o0 = ob[pl.ds(16 * direction, 8), :]
         o1 = ob[pl.ds(16 * direction + 8, 8), :]
         row = lax.broadcasted_iota(jnp.int32, (8, 128), 0)
-        column = lax.broadcasted_iota(jnp.int32, (8, 128), 1) + o0
-        reach = lax.rem(row, 4) + o1
-        number, _ = places(o0, o1, direction)
+        column = lax.broadcasted_iota(jnp.int32, (8, 128), 1)
+        if edge:
+            number = numbers[direction, 8:16]
+            column = column + o0
+            reach = lax.rem(row, 4) + o1
+        else:
+            _, inner, outer, _ = border_cells(o0, o1, direction)
+            number = inner.astype(jnp.int32)
+            numbers[direction, 8:16] = outer.astype(jnp.int32)
+            reach = 2 + lax.rem(row, 4) if direction else -lax.rem(row, 4)
         number_t = jnp.transpose(jnp.concatenate([number, jnp.zeros((120, 128), jnp.int32)], axis=0))
-        slot = lax.broadcasted_iota(jnp.int32, (128, CAP), 1)
+        first = 256 if edge else 0
+        slot = lax.broadcasted_iota(jnp.int32, (128, SLOTS - first), 1) + first
         row16 = lax.broadcasted_iota(jnp.int32, (16, 128), 0)
         cells = []
         for s in range(8):
-            pick[s * 128:(s + 1) * 128, :] = jnp.where(number_t[:, s:s + 1] == slot, 1.0, 0.0).astype(BF16)
+            pick[s * 128:(s + 1) * 128, first:SLOTS] = jnp.where(number_t[:, s:s + 1] == slot, 1.0, 0.0).astype(BF16)
             v = jnp.where(row16 == 0, column[s:s + 1], jnp.where(row16 == 1, reach[s:s + 1], s // 4))
             cells.append(v.astype(F32).astype(BF16))
-        found = jnp.dot(jnp.concatenate(cells, axis=1), pick[...], preferred_element_type=F32)
-        known[direction] = found.astype(jnp.int32)
+        found = jnp.dot(
+            jnp.concatenate(cells, axis=1), pick[:, first:SLOTS], preferred_element_type=F32).astype(jnp.int32)
+        if edge:
+            found = found + known[direction, :, first:SLOTS]
+        known[direction, :, first:SLOTS] = found
 
     def send_packed(direction, c, with_edges):
         here = slice(c * 128, (c + 1) * 128)
@@ -277,8 +315,19 @@
         for hh in range(4):
             w = tap_select(hh + (4 if direction else -4) - reach, LAT_TAPS)
             total = total + w * y[hh * TP:(hh + 1) * TP]
-        zs[direction, c] = total
-        z_copy(direction, c).start()
+        last = c == chunks - 1
+        if last:
+            group = lax.broadcasted_iota(jnp.int32, (REST, 128), 1) // REST
+            rest = total[0:REST]
+            for n in range(1, 4):
+                more = total[n * REST:min((n + 1) * REST, TP)]
+                if more.shape[0] < REST:
+                    more = jnp.concatenate([more, jnp.zeros((REST - more.shape[0], 128), F32)], axis=0)
+                rest = jnp.where(group == n, pltpu.roll(more, n * REST, 1), rest)
+            zs[direction, c, 0:REST] = rest
+        else:
+            zs[direction, c] = total
+        z_copy(direction, c, last).start()
 
     if dense:
         with jax.named_scope("ewait"):
@@ -302,9 +351,10 @@
                 if dense:
                     send_dense(direction)
                 else:
-                    find_cells(direction)
-                    for c in range(CAP // 128 - 1):
+                    find_cells(direction, False)
+                    for c in range(2):
                         send_packed(direction, c, False)
+                    find_cells(direction, True)
 
     if not dense:
         with jax.named_scope("ewait"):
@@ -320,9 +370,10 @@
             @pl.when(has_up if direction else has_down)
             def _():
                 with jax.named_scope("part_edges"):
-                    send_packed(direction, CAP // 128 - 1, True)
-
-        slot = lax.broadcasted_iota(jnp.int32, (CAP, 128), 0)
+                    send_packed(direction, 2, True)
+                    send_packed(direction, 3, True)
+
+        slot = lax.broadcasted_iota(jnp.int32, (SLOTS, 128), 0)
         with jax.named_scope("spread"):
             for direction in range(2):
                 for s in range(8):
@@ -406,9 +457,15 @@
     with jax.named_scope("own_outer"):
         lax.fori_loop(0, 8, lambda pair, _: own(pair, False), 0)
 
-    def add(direction, c):
-        z_copy(direction, c).wait_recv()
-        z = zr[direction, c]
+    def add(direction, c, last=False):
+        z_copy(direction, c, last).wait_recv()
+        if last and not dense:
+            rest = zr[direction, c, 0:REST]
+            z = jnp.concatenate(
+                [rest] + [pltpu.roll(rest, 128 - n * REST, 1)[0:min(REST, TP - n * REST)] for n in range(1, 4)], axis=0)
+            z = jnp.where(lane < REST, z, 0.0)
+        else:
+            z = zr[direction, c]
         if dense:
             lj = (c // 4) * 16 + 12 * direction + lax.rem(c, 4)
             acc[lj] = acc[lj] + z
@@ -421,11 +478,11 @@
             lj = (s // 4) * 16 + 12 * direction + s % 4
             acc[lj] = acc[lj] + (d[0:TP, s * 128:(s + 1) * 128] + d[TP:, s * 128:(s + 1) * 128])
 
-    def add_both(c, _):
+    def add_both(c, _, last=False):
         for direction in range(2):
             @pl.when(has_down if direction else has_up)
             def _():
-                add(direction, c)
+                add(direction, c, last)
         return 0
 
     with jax.named_scope("add"):
@@ -435,7 +492,7 @@
         for c in b_copies[0]:
             c.start()
     with jax.named_scope("add_last"):
-        add_both(chunks - 1, 0)
+        add_both(chunks - 1, 0, True)
 
     with jax.named_scope("square2"):
         ra[1, 0] = row_sums(0)
@@ -478,7 +535,8 @@
         @pl.when(has_up if direction else has_down)
         def _():
             o_copy(1 - direction).wait_send()
-            lax.fori_loop(0, chunks, lambda s, _: (z_copy(direction, s).wait_send(), 0)[1], 0)
+            lax.fori_loop(0, chunks - 1, lambda s, _: (z_copy(direction, s).wait_send(), 0)[1], 0)
+            z_copy(direction, chunks - 1, True).wait_send()
     put_flag.wait()
 
 
@@ -523,9 +581,10 @@
                     pltpu.SMEM((1,), jnp.int32),
                     vmem((2, ZGROUP, 16, 128), F32),
                     vmem((2, nb, 16, 128), F32),
-                    vmem((2, 16, CAP), jnp.int32),
-                    vmem((1024, CAP), BF16),
-                    vmem((2, CAP, 1024), BF16),
+                    vmem((2, 16, 128), jnp.int32),
+                    vmem((2, 16, SLOTS), jnp.int32),
+                    vmem((1024, SLOTS), BF16),
+                    vmem((2, SLOTS, 1024), BF16),
                     vmem((2, 1, 128), F32),
                     vmem((nlat // 2, 1, 128), F32),
                     dma((4,)), dma((2,)), dma((2,)), dma((2,)), dma((2,)), dma((2, 8)), dma((2, 8)),

time: 47.7 us -> 45 us (0.943)
  Pallas kernels: 45.8 us -> 42.9 us
    pallas_call x1, Pallas kernels: 45.8 us -> 42.9 us  [run(): pl.pallas_call(functools.partial(kernel, dense, nt, nlat, nlon), out_shap...]
where the time goes in v5:
time: 45 us; the launch traced here: 44.9 us
  Pallas kernels  42.9 us (95%)
  local copies, waits for them, and re-layouts  1.17 us (3%)
  between operations  0.63 us (1%)
    pallas_call x1, Pallas kernels, run(): pl.pallas_call(functools.partial(kernel, dense, nt, nlat, nlon), out_shap...  42.9 us
    unnamed x1, local copies, waits for them, and re-layouts  1.17 us

profile of v5, /device:TPU:1, one launch (start us, length us, event | category | flops | bytes accessed | tf_op | source)
XLA Modules:
  0.0 44.9 jit_solution(3382106527313267372)
XLA Ops:
  0.0 42.9 %shard_map.48 = (f32[3200,128]{1,0:T(8,128)S(1)}, s32[1]{0:T(128)}) custom-call(f32[100,32,128]{2,1,0:T(8,128)} %bitcast.8, s32[64,128]{1,0:T(8,128)} %bitcast.12, f32[32,100]{1,0:T(8,128)} %bitcast.14, s32[16]{0:T(128)} %mask_hbm.1), custom_call_target="tpu_custom_call" | custom-call | tf_op jit(solution)/shard_map/pallas_call | solution.py:558
  43.5 0.2 conditional.1
  43.7 1.2 %copy.11 = f32[100,2,16,128]{3,2,1,0:T(8,128)} copy(f32[100,2,16,128]{3,2,1,0:T(8,128)S(1)} %get-tuple-element.28) | data formatting | bytes 3276800

commit v6 on v5

--- a/solution.py
+++ b/solution.py
@@ -20,8 +20,8 @@
 PITCH = 40
 STEP = 4
 SLOTS = 512
-CAP = 416
-REST = 32
+CAP = 400
+REST = 16
 FLAG = 120
 
 
@@ -241,6 +241,13 @@
                 device_id=x_peer(k) if k else {"lat": lat + 1 - 2 * lax.rem(lat, 2)}, device_id_type=MESH))
         f_copies[0].start()
 
+        slot = lax.broadcasted_iota(jnp.int32, (SLOTS, 128), 0)
+        with jax.named_scope("spread"):
+            for direction in range(2):
+                for s in range(8):
+                    spread[direction, :, s * 128:(s + 1) * 128] = jnp.where(
+                        place[direction][s:s + 1] == slot, 1.0, 0.0).astype(BF16)
+
     def edges(first, step):
         for i in range(STEP):
             lj = 16 * (step // 2) + first + (4 if first else 12) * lax.rem(step, 2) + i
@@ -319,10 +326,8 @@
         if last:
             group = lax.broadcasted_iota(jnp.int32, (REST, 128), 1) // REST
             rest = total[0:REST]
-            for n in range(1, 4):
-                more = total[n * REST:min((n + 1) * REST, TP)]
-                if more.shape[0] < REST:
-                    more = jnp.concatenate([more, jnp.zeros((REST - more.shape[0], 128), F32)], axis=0)
+            for n in range(1, TP // REST):
+                more = total[n * REST:(n + 1) * REST]
                 rest = jnp.where(group == n, pltpu.roll(more, n * REST, 1), rest)
             zs[direction, c, 0:REST] = rest
         else:
@@ -373,13 +378,6 @@
                     send_packed(direction, 2, True)
                     send_packed(direction, 3, True)
 
-        slot = lax.broadcasted_iota(jnp.int32, (SLOTS, 128), 0)
-        with jax.named_scope("spread"):
-            for direction in range(2):
-                for s in range(8):
-                    spread[direction, :, s * 128:(s + 1) * 128] = jnp.where(
-                        place[direction][s:s + 1] == slot, 1.0, 0.0).astype(BF16)
-
         f_copies[0].wait_recv()
         fs[1] = fs[0] + fr[0]
         for c in f_copies[1:]:
@@ -452,8 +450,6 @@
             lj = 16 * (n // 8) + first + (n % 8 if first else n % 8 + 8 * (n % 8 // 4))
             out_ref[pl.ds(lj, nt, stride=32), :] = acc[lj, 0:nt]
 
-    save_rows(4)
-
     with jax.named_scope("own_outer"):
         lax.fori_loop(0, 8, lambda pair, _: own(pair, False), 0)
 
@@ -461,8 +457,7 @@
         z_copy(direction, c, last).wait_recv()
         if last and not dense:
             rest = zr[direction, c, 0:REST]
-            z = jnp.concatenate(
-                [rest] + [pltpu.roll(rest, 128 - n * REST, 1)[0:min(REST, TP - n * REST)] for n in range(1, 4)], axis=0)
+            z = jnp.concatenate([rest] + [pltpu.roll(rest, 128 - n * REST, 1) for n in range(1, TP // REST)], axis=0)
             z = jnp.where(lane < REST, z, 0.0)
         else:
             z = zr[direction, c]
@@ -498,6 +493,7 @@
         ra[1, 0] = row_sums(0)
     for c in a_copies[1]:
         c.start()
+    save_rows(4)
     save_rows(0)
     with jax.named_scope("exA"):
         rb[1, 0] = total_of(a_copies[1], ra.at[1])

time: 45 us -> 44.4 us (0.987)
  Pallas kernels: 42.9 us -> 42.3 us
    pallas_call x1, Pallas kernels: 42.9 us -> 42.3 us  [run(): pl.pallas_call(functools.partial(kernel, dense, nt, nlat, nlon), out_shap...]
where the time goes in v6:
time: 44.4 us; the launch traced here: 44.3 us
  Pallas kernels  42.3 us (95%)
  local copies, waits for them, and re-layouts  1.17 us (3%)
  between operations  0.63 us (1%)
    pallas_call x1, Pallas kernels, run(): pl.pallas_call(functools.partial(kernel, dense, nt, nlat, nlon), out_shap...  42.3 us
    unnamed x1, local copies, waits for them, and re-layouts  1.17 us

profile of v6, /device:TPU:1, one launch (start us, length us, event | category | flops | bytes accessed | tf_op | source)
XLA Modules:
  0.0 44.3 jit_solution(1359212403044103344)
XLA Ops:
  0.0 42.3 %shard_map.48 = (f32[3200,128]{1,0:T(8,128)S(1)}, s32[1]{0:T(128)}) custom-call(f32[100,32,128]{2,1,0:T(8,128)} %bitcast.8, s32[64,128]{1,0:T(8,128)} %bitcast.12, f32[32,100]{1,0:T(8,128)} %bitcast.14, s32[16]{0:T(128)} %mask_hbm.1), custom_call_target="tpu_custom_call" | custom-call | tf_op jit(solution)/shard_map/pallas_call | solution.py:554
  42.9 0.2 conditional.1
  43.1 1.2 %copy.11 = f32[100,2,16,128]{3,2,1,0:T(8,128)} copy(f32[100,2,16,128]{3,2,1,0:T(8,128)S(1)} %get-tuple-element.28) | data formatting | bytes 3276800

commit v7 on v6

--- a/solution.py
+++ b/solution.py
@@ -106,7 +106,7 @@
     load_x = pltpu.make_async_copy(
         x_hbm, xv.reshape(TP, PITCH, 128).at[pl.ds(0, nt), pl.ds(0, 32), :], local_sem.at[0])
     load_x.start()
-    load_off = pltpu.make_async_copy(off_hbm, offv, local_sem.at[1])
+    load_off = pltpu.make_async_copy(off_hbm, offv.at[pl.ds(0, 64)], local_sem.at[1])
     load_off.start()
     load_target = pltpu.make_async_copy(target_hbm, target_v, local_sem.at[2])
     load_target.start()
@@ -163,11 +163,11 @@
             barrier,
             has_up.astype(jnp.int32) + has_down.astype(jnp.int32) + nlat // 2 + 1 + (ZGROUP - 1) + (ny * CORES - 1))
 
-    ob4 = ob.reshape(2, 2, 2, 4, 128)
+    ob4 = ob.at[pl.ds(0, 32)].reshape(2, 2, 2, 4, 128)
 
     def o_copy(direction):
         return pltpu.make_async_remote_copy(
-            src_ref=offv.reshape(2, 2, 16, 128).at[:, :, pl.ds(12 * direction, 4), :],
+            src_ref=offv.at[pl.ds(0, 64)].reshape(2, 2, 16, 128).at[:, :, pl.ds(12 * direction, 4), :],
             dst_ref=ob4.at[direction],
             send_sem=o_send.at[direction], recv_sem=o_recv.at[direction],
             device_id={"lat": lat - 1 + 2 * direction}, device_id_type=MESH)
@@ -448,7 +448,7 @@
     def save_rows(first):
         for n in range(16):
             lj = 16 * (n // 8) + first + (n % 8 if first else n % 8 + 8 * (n % 8 // 4))
-            out_ref[pl.ds(lj, nt, stride=32), :] = acc[lj, 0:nt]
+            out_ref[pl.ds(lj, TP, stride=32), :] = acc[lj]
 
     with jax.named_scope("own_outer"):
         lax.fori_loop(0, 8, lambda pair, _: own(pair, False), 0)
@@ -554,7 +554,7 @@
             return pl.pallas_call(
                 functools.partial(kernel, dense, nt, nlat, nlon),
                 out_shape=[
-                    jax.ShapeDtypeStruct((nt * 32, 128), F32),
+                    jax.ShapeDtypeStruct((TP * 32, 128), F32),
                     jax.ShapeDtypeStruct((1,), jnp.int32),
                 ],
                 in_specs=[pl.BlockSpec(memory_space=pltpu.HBM)] * 4,
@@ -562,12 +562,12 @@
                 scratch_shapes=[
                     vmem((TP * PITCH, 128), F32),
                     vmem((2 * BANDS * TP, KW), BF16),
-                    vmem((64, 128), jnp.int32),
+                    vmem((72, 128), jnp.int32),
                     vmem((32, nt), F32),
                     pltpu.SMEM((16,), jnp.int32),
                     vmem((2, TP, 128), F32),
                     vmem((2, TP, 128), F32),
-                    vmem((32, 128), jnp.int32),
+                    vmem((40, 128), jnp.int32),
                     vmem((2, 8, TP, 128), F32),
                     vmem((2, 8, TP, 128), F32),
                     vmem((32, TP, 128), F32),
@@ -593,7 +593,7 @@
 
         out, flag = run(False)
         out = lax.cond(flag[0] > 0, lambda: run(True)[0], lambda: out)
-        return out.reshape(tracers.shape)
+        return out[0:nt * 32].reshape(tracers.shape)
 
     placed = (
         P(None, None, "lat", "lon"),

time: 44.4 us -> 44.5 us (level)
    unnamed x1 -> x2, local copies, waits for them, and re-layouts: 1.17 us -> 1.16 us
where the time goes in v7:
time: 44.5 us; the launch traced here: 44.4 us
  Pallas kernels  42.3 us (95%)
  local copies, waits for them, and re-layouts  1.27 us (3%)
  between operations  0.64 us (1%)
    pallas_call x1, Pallas kernels, run(): pl.pallas_call(functools.partial(kernel, dense, nt, nlat, nlon), out_shap...  42.3 us
    unnamed x2, local copies, waits for them, and re-layouts  1.16 us

profile of v7, /device:TPU:1, one launch (start us, length us, event | category | flops | bytes accessed | tf_op | source)
XLA Modules:
  0.0 44.4 jit_solution(17676170517937028946)
XLA Ops:
  0.0 42.3 %shard_map.48 = (f32[3584,128]{1,0:T(8,128)S(1)}, s32[1]{0:T(128)}) custom-call(f32[100,32,128]{2,1,0:T(8,128)} %bitcast.8, s32[64,128]{1,0:T(8,128)} %bitcast.12, f32[32,100]{1,0:T(8,128)} %bitcast.14, s32[16]{0:T(128)} %mask_hbm.1), custom_call_target="tpu_custom_call" | custom-call | tf_op jit(solution)/shard_map/pallas_call | solution.py:554
  42.9 0.3 conditional.1
  42.9 0.1 slice.5
  43.3 0.0 copy-start
  43.3 1.2 %copy-done = f32[100,2,16,128]{3,2,1,0:T(8,128)} copy-done((f32[100,2,16,128]{3,2,1,0:T(8,128)}, f32[100,2,16,128]{3,2,1,0:T(8,128)S(1)}, u32[]{:S(2)}) %copy-start) | copy-done | bytes 1638424
Async XLA Ops:
  43.3 1.2 %copy-start = (f32[100,2,16,128]{3,2,1,0:T(8,128)}, f32[100,2,16,128]{3,2,1,0:T(8,128)S(1)}, u32[]{:S(2)}) copy-start(f32[100,2,16,128]{3,2,1,0:T(8,128)S(1)} %get-tuple-element.31) | copy-start | bytes 4915204
